TPU v7x, 256 devices: a whole 4x4x8 slice. The times are simulated.
256 devices in a mesh: ep: 64 (over z, y, core), fsdp: 4 (over x).
Axes of the slice: x: 4, y: 4, z: 8, core: 2. Of those that a mesh axis runs over, the one named last changes fastest.
Arguments:
- w_down: float32 [64, 1408, 2048], P('ep', None, 'fsdp'), may hold values from -0.21875 to 0.21875
- avg_down: float32 [64, 1408, 2048], P('ep', None, 'fsdp'), may hold values from -0.15625 to 0.15625
- router_weight: float32 [2048, 64], P('fsdp', 'ep'), may hold values from -0.125 to 0.125
- router_gain: float32 [2048], P('fsdp'), may hold values from 0.25 to 1.75
Outputs:
- serve_down: bfloat16 [64, 1408, 2048], P('ep')
- scale_down: float32 [64, 1408], P('ep')
- serve_router: bfloat16 [2048, 64], replicated
- fresh_down: float32 [64, 1408, 2048], P('ep', None, 'fsdp')
All inputs are finite; a program needn't handle non-finite values. Where the computation divides by a largest or mean magnitude, that divisor is 1e-20 or more.
Results may differ from a plain program's by a relative error of at most 0.001.
Values may be sent and summed in bfloat16 or wider, within the bound.
No kernel may reach another device: no remote copies, remote signals or barrier semaphores. Data moves between devices by JAX's collectives and lax.ppermute only.
A program may use at most 64 MiB of HBM per device.

v0:
```python
import jax
import jax.numpy as jnp
from jax import lax
from jax.sharding import PartitionSpec as P


def sent_to_all(value, axis):
    copies = jnp.broadcast_to(value, (lax.axis_size(axis), *value.shape))
    return lax.all_to_all(copies, axis, split_axis=0, concat_axis=0, tiled=True)


def of_everyone(value, axis):
    everything = sent_to_all(value, axis)
    return jnp.max(everything, axis=0)


def in_order(blocks, dim):
    blocks = jnp.moveaxis(blocks, 0, dim)
    dims = blocks.shape
    return blocks.reshape(*dims[:dim], dims[dim] * dims[dim + 1], *dims[dim + 2 :])


def collect(value, axis, dim):
    return in_order(sent_to_all(value, axis), dim)


def body(w_down, avg_down, router_weight, router_gain):
    fresh_down = 0.5 * avg_down + 0.5 * w_down
    scale_down = of_everyone(jnp.max(jnp.abs(fresh_down), axis=2), "fsdp")
    narrow_down = (fresh_down / jnp.expand_dims(scale_down, 2)).astype(jnp.bfloat16)
    serve_down = lax.all_gather(narrow_down, "fsdp", axis=2, tiled=True)
    part_router = (router_weight * router_gain[:, None]).astype(jnp.bfloat16)
    row_router = lax.all_gather(part_router, "fsdp", axis=0, tiled=True)
    serve_router = collect(row_router, "ep", 1)
    return (serve_down, scale_down, serve_router, fresh_down)


def solution(mesh):
    placed = (P("ep", None, "fsdp"), P("ep", None, "fsdp"), P("fsdp", "ep"), P("fsdp"))
    return jax.shard_map(
        body,
        mesh=mesh,
        in_specs=placed,
        out_specs=(P("ep", None, None), P("ep", None), P(), P("ep", None, "fsdp")),
        check_vma=False,
    )
```

profile of v0, /device:TPU:1, one launch (start us, length us, event | category | flops | bytes accessed | tf_op | source)
XLA Modules:
  0.0 100.1 jit_solution(13331226451269503026)
XLA Ops:
  7.2 0.0 all-gather.2.cloned.1.call-start
  7.2 3.2 %abs_reduce_fusion = (f32[1408]{0:T(1024)S(1)}, f32[1,1408,512]{2,1,0:T(8,128)S(1)}) fusion(f32[1,1408,512]{2,1,0:T(8,128)} %param.5, f32[1,1408,512]{2,1,0:T(8,128)} %param.4), kind=kLoop, calls=%fused_computation.1 | loop fusion | flops 2882176 | bytes 8656384 | tf_op jit(solution)/shard_map/reduce_max | solution.py:29
  10.4 0.0 copy-start
  10.4 8.9 %all_to_all.10 = f32[4,1,1408]{2,1,0:T(1,128)S(1)} all-to-all(f32[4,1,1408]{2,1,0:T(1,128)S(1)} %broadcast_in_dim.10), channel_id=1, replica_groups=mesh['ep'=64,'fsdp'=4] {'fsdp'}, dimensions={0} | all-to-all | bytes 45056 | tf_op jit(solution)/shard_map/all_to_all | solution.py:9
  19.3 0.0 copy-start.1
  19.3 0.0 copy-start.2
  19.3 1.4 %divide_convert_fusion = bf16[1,1408,512]{2,1,0:T(8,128)(2,1)} fusion(f32[1,1408,512]{2,1,0:T(8,128)S(1)} %get-tuple-element.13, f32[1408]{0:T(1024)S(1)} %reduce_max.21), kind=kLoop, calls=%fused_computation | loop fusion | flops 1441792 | bytes 4331008 | tf_op jit(solution)/shard_map/convert_element_type | solution.py:30
  20.7 0.0 all-gather.2.cloned.1.call-update
  20.7 0.0 copy-done
  20.7 0.0 copy-done.1
  20.7 0.0 copy-done.2
  20.8 8.1 %all_gather.9 = bf16[2048,1]{0,1:T(2,128)(2,1)S(1)} all-gather(bf16[512,1]{0,1:T(2,128)(2,1)S(1)} %multiply_convert_fusion), channel_id=1, replica_groups=mesh['ep'=64,'fsdp'=4] {'fsdp'}, dimensions={0}, use_global_device_ids=true | all-gather | bytes 5120 | tf_op jit(solution)/shard_map/all_gather | solution.py:33
  28.9 0.3 broadcast_bitcast_fusion
  29.2 0.5 broadcast.12
  29.7 2.2 %reduce.3 = bf16[64,2048]{1,0:T(8,128)(2,1)S(1)} reduce(bf16[64,1,2048]{2,1,0:T(2,128)(2,1)S(1)} %broadcast_bitcast_fusion, bf16[]{:T(256)} %broadcast.12), dimensions={1}, to_apply=%broadcast_bitcast_fusion.reduce_sub_computation | reduce | bytes 524290
  31.9 0.9 reshape.22
  32.8 16.1 %all-to-all-start.1 = ((bf16[64,2,1024]{2,1,0:T(2,128)(2,1)}), bf16[64,2,1024]{2,1,0:T(2,128)(2,1)S(1)}, u32[]{:S(2)}, u32[]{:S(2)}) async-start(bf16[64,2,1024]{2,1,0:T(2,128)(2,1)} %reshape.22), calls=%async_computation.1 | async-start | bytes 524288 | tf_op jit(solution)/shard_map/all_to_all | solution.py:9
  48.8 0.6 reduce_max.22
  49.4 12.5 %all-to-all-done.1 = bf16[64,2,1024]{2,1,0:T(2,128)(2,1)S(1)} async-done(((bf16[64,2,1024]{2,1,0:T(2,128)(2,1)}), bf16[64,2,1024]{2,1,0:T(2,128)(2,1)S(1)}, u32[]{:S(2)}, u32[]{:S(2)}) %all-to-all-start.1) | async-done | bytes 262176 | tf_op jit(solution)/shard_map/all_to_all | solution.py:9
  61.9 0.2 reshape.23
  62.2 0.9 copy.14
  63.0 24.1 %all-gather.2.cloned.1.call-done = bf16[1,1408,2048]{2,1,0:T(8,128)(2,1)} async-done(((bf16[1,1408,512]{2,1,0:T(8,128)(2,1)}), bf16[1,1408,2048]{2,1,0:T(8,128)(2,1)}) %all-gather.2.cloned.1.call-update) | async-done | bytes 5767184 | tf_op jit(solution)/shard_map/all_gather | solution.py:31
  87.1 6.2 %copy.16 = bf16[1,1408,2048]{2,1,0:T(8,128)(2,1)} copy(bf16[1,1408,2048]{2,1,0:T(8,128)(2,1)} %all-gather.2.cloned.1.call-done) | data formatting | bytes 11534336
  (4 shorter events, 0.1 us)
Async XLA Ops:
  7.2 79.9 %all-gather.2.cloned.1.call-start = ((), (), s32[]{:S(2)}) async-start(), calls=%async_computation.2 | async-start | bytes 7208960 | tf_op jit(solution)/shard_map/all_gather | solution.py:31
  10.4 10.4 %copy-start = (f32[1,1408,512]{2,1,0:T(8,128)}, f32[1,1408,512]{2,1,0:T(8,128)S(1)}, u32[]{:S(2)}) copy-start(f32[1,1408,512]{2,1,0:T(8,128)S(1)} %get-tuple-element.13) | copy-start | bytes 8650756
  19.3 1.4 %copy-start.1 = (f32[512,1]{0,1:T(1,128)S(1)}, f32[512,1]{0,1:T(1,128)}, u32[]{:S(2)}) copy-start(f32[512,1]{0,1:T(1,128)} %param.6) | copy-start | bytes 6148
  19.3 1.4 %copy-start.2 = (f32[512]{0:T(512)S(1)}, f32[512]{0:T(512)}, u32[]{:S(2)}) copy-start(f32[512]{0:T(512)} %param.7) | copy-start | bytes 6148
  32.8 29.1 %all-to-all-start.1 = ((bf16[64,2,1024]{2,1,0:T(2,128)(2,1)}), bf16[64,2,1024]{2,1,0:T(2,128)(2,1)S(1)}, u32[]{:S(2)}, u32[]{:S(2)}) async-start(bf16[64,2,1024]{2,1,0:T(2,128)(2,1)} %reshape.22), calls=%async_computation.1 | async-start | bytes 524288 | tf_op jit(solution)/shard_map/all_to_all | solution.py:9
Sparse Core Ops, SparseCore 0:
  20.8 66.1 all-gather.1
where the time goes:
time: 100 us
  waiting for transfers between devices  36.5 us (36%)
  blocking collectives  17 us (17%)
  starting transfers between devices  16.1 us (16%)
  between operations  14.1 us (14%)
  local copies, waits for them, and re-layouts  9.53 us (10%)
  other arithmetic  6.74 us (7%)
    all_gather x1, waiting for transfers between devices, body(): serve_down = lax.all_gather(narrow_down, 'fsdp', axis=2, tiled=True)  24.1 us
    all_to_all x1, starting transfers between devices, sent_to_all(): return lax.all_to_all(copies, axis, split_axis=0, concat_axis=0, tiled=True)  16.1 us
    all_to_all x1, waiting for transfers between devices, sent_to_all(): return lax.all_to_all(copies, axis, split_axis=0, concat_axis=0, tiled=True)  12.5 us
    all_to_all x1, blocking collectives, sent_to_all(): return lax.all_to_all(copies, axis, split_axis=0, concat_axis=0, tiled=True)  8.88 us
    all_gather x1, blocking collectives, body(): row_router = lax.all_gather(part_router, 'fsdp', axis=0, tiled=True)  8.14 us
    unnamed x11, local copies, waits for them, and re-layouts  8.06 us
    reduce_max x1, other arithmetic, body(): scale_down = of_everyone(jnp.max(jnp.abs(fresh_down), axis=2), 'fsdp')  3.15 us
    unnamed x1, other arithmetic  2.15 us
  transfers between devices with their start and end apart: 2, of which 2 were waited for; matrix products, arithmetic and copies ran while one was open for 6% of the time, Pallas kernels for 0%

commit v1 on v0

v1 whole, which is shorter than its diff:
```python
import functools

import jax
import jax.numpy as jnp
from jax import lax
from jax.experimental import pallas as pl
from jax.experimental.pallas import tpu as pltpu
from jax.sharding import PartitionSpec as P


F32, BF16 = jnp.float32, jnp.bfloat16
ANY = pl.BlockSpec(memory_space=pl.ANY)
VM = pl.BlockSpec(memory_space=pltpu.VMEM)
LANES = 128
HALF = LANES // 2
CORES, YS, ZS = 2, 4, 8
RING = (0, 1, 3, 2)
TOWER = (0, 1, 2, 3, 7, 6, 5, 4)


def in_vmem(x):
    return pltpu.with_memory_space_constraint(x, pltpu.VMEM)


def in_hbm(x):
    return pltpu.with_memory_space_constraint(x, pltpu.HBM)


def call(kernel, ins, in_specs, outs, out_specs, scratch=(), aliases=None):
    return pl.pallas_call(
        kernel,
        out_shape=outs,
        in_specs=in_specs,
        out_specs=out_specs,
        scratch_shapes=list(scratch),
        input_output_aliases=aliases or {},
        compiler_params=pltpu.CompilerParams(vmem_limit_bytes=40 * 1024 * 1024),
    )(*ins)


def run(copies):
    for copy in copies:
        copy.start()
    for copy in copies:
        copy.wait()


def fresh_kernel(groups, w_hbm, a_hbm, rw_hbm, rg_hbm, fresh_ref, msg_ref, w_buf, a_buf, r_buf, sems, r_sems):
    def copies(g):
        rows = pl.ds(g * LANES, LANES)
        return (
            pltpu.make_async_copy(w_hbm.at[0, rows, :], w_buf.at[rows, :], sems.at[0, g]),
            pltpu.make_async_copy(a_hbm.at[0, rows, :], a_buf.at[rows, :], sems.at[1, g]),
        )

    router = [
        pltpu.make_async_copy(rw_hbm, r_buf.at[0:1, :], r_sems.at[0]),
        pltpu.make_async_copy(rg_hbm, r_buf.at[1:2, :], r_sems.at[1]),
    ]
    for g in range(groups):
        for copy in copies(g):
            copy.start()
    for copy in router:
        copy.start()
    for g in range(groups):
        for copy in copies(g):
            copy.wait()
        rows = slice(g * LANES, (g + 1) * LANES)
        fresh = 0.5 * a_buf[rows, :] + 0.5 * w_buf[rows, :]
        fresh_ref[rows, :] = fresh
        size = jnp.abs(fresh)
        top = size[:, :LANES]
        for k in range(1, size.shape[1] // LANES):
            top = jnp.maximum(top, size[:, k * LANES : (k + 1) * LANES])
        msg_ref[g : g + 1, :] = jnp.max(top.T, axis=0, keepdims=True)
    for copy in router:
        copy.wait()
    part = r_buf[0:1, :] * r_buf[1:2, :]
    for k in range(part.shape[1] // LANES):
        msg_ref[groups + k : groups + k + 1, :] = part[:, k * LANES : (k + 1) * LANES]


def serve_kernel(groups, fresh_ref, m0, m1, a_ref, b_ref, scale_ref):
    scale_ref[...] = jnp.maximum(m0[:groups, :], m1[:groups, :])
    rows = a_ref.shape[0]
    for g in range(groups):
        inverse = 1.0 / scale_ref[g : g + 1, :]
        spread = jnp.broadcast_to(inverse, (LANES, LANES)).T
        for h in (0, 1):
            row = g * LANES + h * HALF
            out, at = (a_ref, row) if row < rows else (b_ref, row - rows)
            factor = spread[h * HALF : (h + 1) * HALF, :]
            for k in range(fresh_ref.shape[1] // LANES):
                lanes = slice(k * LANES, (k + 1) * LANES)
                out[at : at + HALF, lanes] = (fresh_ref[row : row + HALF, lanes] * factor).astype(BF16)


def spot(piece, out, back, row, sem):
    xs = lax.axis_size("fsdp")
    owner = lax.rem(lax.axis_index("fsdp") + (xs - back), xs)
    width = piece.shape[1]
    cols = pl.ds(pl.multiple_of(owner * width, width), width)
    return pltpu.make_async_copy(piece, out.at[0, pl.ds(row, piece.shape[0]), cols], sem)


def own_kernel(groups, a_ref, b_ref, fresh_ref, scale_ref, out, fresh_out, scale_out, line, sems):
    for g in range(groups):
        line[:, g * LANES : (g + 1) * LANES] = scale_ref[g : g + 1, :]
    run([
        spot(a_ref, out, 0, 0, sems.at[0]),
        spot(b_ref, out, 0, a_ref.shape[0], sems.at[1]),
        pltpu.make_async_copy(fresh_ref, fresh_out.at[0], sems.at[2]),
        pltpu.make_async_copy(line, scale_out, sems.at[3]),
    ])


def place_kernel(spots, *refs):
    n = len(spots)
    pieces, out, sems = refs[:n], refs[-2], refs[-1]
    run([spot(piece, out, back, row, sems.at[i]) for i, (piece, (back, row)) in enumerate(zip(pieces, spots))])


def place(out, pieces, spots):
    ins = [in_vmem(p) for p in pieces] + [out]
    return call(
        functools.partial(place_kernel, tuple(spots)),
        ins, [VM] * len(pieces) + [ANY], pltpu.HBM(out.shape, out.dtype), ANY,
        [pltpu.SemaphoreType.DMA((len(pieces),))], {len(pieces): 0},
    )


def router_rows_kernel(part, lines, out, buf):
    x, e = lax.axis_index("fsdp"), lax.axis_index("ep")
    y, c = lax.rem(e // CORES, YS), lax.rem(e, CORES)
    xs = lax.axis_size("fsdp")
    at = 0
    for yk in RING:
        for ck in range(CORES):
            row = CORES * (y ^ yk) + (c ^ ck)
            for xk in RING:
                for k in range(part):
                    buf[pl.ds((row * xs + (x ^ xk)) * part + k, 1), :] = lines[at : at + 1, :]
                    at += 1
    for j in range(xs * part):
        out[:, j * LANES : (j + 1) * LANES] = buf[pl.ds(j, CORES * YS, stride=xs * part), :].astype(BF16)


def router_place_kernel(*refs):
    pieces, out, sems = refs[:-2], refs[-2], refs[-1]
    per = CORES * YS
    z = lax.axis_index("ep") // per
    copies = []
    for piece in pieces:
        for k in range(piece.shape[0] // per):
            owner = z ^ TOWER[len(copies)]
            rows = pl.ds(pl.multiple_of(owner * per, per), per)
            copies.append(pltpu.make_async_copy(piece.at[pl.ds(k * per, per), :], out.at[rows, :], sems.at[len(copies)]))
    run(copies)


def body(w_down, avg_down, router_weight, router_gain):
    _, rows, cols = w_down.shape
    groups, half = rows // LANES, rows // 2
    xs, eps = lax.axis_size("fsdp"), lax.axis_size("ep")
    per, part = CORES * YS, cols // LANES

    def move(v, axis, to):
        return lax.ppermute(v, axis, [(i, to(i)) for i in range(lax.axis_size(axis))])

    def shift(v, by):
        return move(v, "fsdp", lambda i: (i + by) % xs)

    def swap(v, step):
        return jnp.concatenate([v, move(v, "ep", lambda e: e ^ step)], 0)

    fresh, msg = call(
        functools.partial(fresh_kernel, groups),
        (in_hbm(w_down), in_hbm(avg_down), in_hbm(router_weight.reshape(1, -1)), in_hbm(router_gain.reshape(1, -1))),
        [ANY] * 4,
        (pltpu.VMEM((rows, cols), F32), pltpu.VMEM((groups + part, LANES), F32)),
        (VM, VM),
        [
            pltpu.VMEM((rows, cols), F32), pltpu.VMEM((rows, cols), F32), pltpu.VMEM((2, cols), F32),
            pltpu.SemaphoreType.DMA((2, groups)), pltpu.SemaphoreType.DMA((2,)),
        ],
    )
    other = move(msg, "fsdp", lambda i: i ^ 1)
    msg = jnp.concatenate([jnp.maximum(msg[:groups], other[:groups]), msg[groups:], other[groups:]], 0)
    other = move(msg, "fsdp", lambda i: i ^ 3)
    a, b, scale = call(
        functools.partial(serve_kernel, groups),
        (in_vmem(fresh), in_vmem(msg), in_vmem(other)), [VM] * 3,
        (pltpu.VMEM((half, cols), BF16), pltpu.VMEM((half, cols), BF16), pltpu.VMEM((groups, LANES), F32)), (VM,) * 3,
    )
    a_r, b_l = shift(a, 1), shift(b, -1)
    b_r, a_l = shift(b, 1), shift(a, -1)
    a_rr, b_ll = shift(a_r, 1), shift(b_l, -1)

    out, fresh_out, scale_out = call(
        functools.partial(own_kernel, groups),
        [in_vmem(v) for v in (a, b, fresh, scale)], [VM] * 4,
        (pltpu.HBM((1, rows, cols * xs), BF16), pltpu.HBM((1, rows, cols), F32), pltpu.HBM((1, rows), F32)), (ANY,) * 3,
        [pltpu.VMEM((1, rows), F32), pltpu.SemaphoreType.DMA((4,))],
    )
    out = place(out, [a_r, b_l], [(1, 0), (3, half)])
    out = place(out, [b_r, a_l], [(1, half), (3, 0)])
    out = place(out, [a_rr, b_ll], [(2, 0), (2, half)])

    lines = jnp.concatenate([msg[groups:], other[groups:]], 0)
    lines = swap(lines, 1)
    lines = swap(lines, CORES)
    lines = swap(lines, CORES * 3)
    block = call(
        functools.partial(router_rows_kernel, part),
        [in_vmem(lines)], [VM],
        pltpu.VMEM((per, cols * xs), BF16), VM, [pltpu.VMEM((per * xs * part, LANES), F32)],
    )
    two = move(block, "ep", lambda e: e ^ per)
    both = jnp.concatenate([block, two], 0)
    four = move(both, "ep", lambda e: e ^ (per * 2))
    both = jnp.concatenate([both, four], 0)
    eight = move(both, "ep", lambda e: e ^ (per * 7))
    router = call(
        router_place_kernel,
        [in_vmem(both), in_vmem(eight)], [VM] * 2,
        pltpu.HBM((eps, cols * xs), BF16), ANY, [pltpu.SemaphoreType.DMA((ZS,))],
    )
    return out, scale_out, router.T, fresh_out


def solution(mesh):
    placed = (P("ep", None, "fsdp"), P("ep", None, "fsdp"), P("fsdp", "ep"), P("fsdp"))
    return jax.shard_map(
        body,
        mesh=mesh,
        in_specs=placed,
        out_specs=(P("ep", None, None), P("ep", None), P(), P("ep", None, "fsdp")),
        check_vma=False,
    )
```

time: 100 us -> 71.1 us (0.71)
  the two profiles are of different devices: /device:TPU:1 before, /device:TPU:24 now
where the time goes in v1:
time: 71.1 us; the launch traced here: 70.9 us
  starting transfers between devices  28.5 us (40%)
  waiting for transfers between devices  25.7 us (36%)
  Pallas kernels  15.8 us (22%)
  between operations  0.74 us (1%)
    ppermute x14, starting transfers between devices, move(): lax.ppermute(v, axis, [(i, to(i)) for i in range(lax.axis_size(axis))])  28.5 us
    ppermute x14, waiting for transfers between devices, move(): lax.ppermute(v, axis, [(i, to(i)) for i in range(lax.axis_size(axis))])  25.7 us
    pallas_call x8, Pallas kernels, call(): pl.pallas_call(kernel, out_shape=outs, in_specs=in_specs, out_specs=out_s...  15.8 us
  transfers between devices with their start and end apart: 14, of which 8 were waited for; matrix products, arithmetic and copies ran while one was open for 0% of the time, Pallas kernels for 13%

profile of v1, /device:TPU:24, one launch (start us, length us, event | category | flops | bytes accessed | tf_op | source)
XLA Modules:
  0.0 70.9 jit_solution(5253841262752452433)
XLA Ops:
  0.6 3.0 %shard_map.75 = (f32[1408,512]{1,0:T(8,128)S(1)}, f32[15,128]{1,0:T(8,128)S(1)}) custom-call(f32[1,1408,512]{2,1,0:T(8,128)} %w_hbm.1, f32[1,1408,512]{2,1,0:T(8,128)} %a_hbm.1, f32[1,512]{1,0:T(1,128)} %bitcast.4, f32[1,512]{1,0:T(1,128)} %bitcast.5), custom_call_target="tpu_custom_call" | custom-call | tf_op jit(solution)/shard_map/pallas_call | solution.py:30
  3.6 1.6 %collective-permute-start = (f32[15,128]{1,0:T(8,128)S(1)}, f32[15,128]{1,0:T(8,128)S(1)}, u32[]{:S(2)}, u32[]{:S(2)}) collective-permute-start(f32[15,128]{1,0:T(8,128)S(1)} %get-tuple-element.13), channel_id=1, source_target_pairs={{0,1},{1,0},{2,3},{3,2},{4,5},{5,4},{6,7},{7,6},{8,9},{9,8},{10,11... | collective-permute-start | bytes 23048 | tf_op jit(solution)/shard_map/ppermute | solution.py:168
  5.2 2.2 %collective-permute-done = f32[15,128]{1,0:T(8,128)S(1)} collective-permute-done((f32[15,128]{1,0:T(8,128)S(1)}, f32[15,128]{1,0:T(8,128)S(1)}, u32[]{:S(2)}, u32[]{:S(2)}) %collective-permute-start) | collective-permute-done | bytes 7712 | tf_op jit(solution)/shard_map/ppermute | solution.py:168
  7.3 2.8 %collective-permute-start.1 = (f32[19,128]{1,0:T(8,128)S(1)}, f32[19,128]{1,0:T(8,128)S(1)}, u32[]{:S(2)}, u32[]{:S(2)}) collective-permute-start(f32[19,128]{1,0:T(8,128)S(1)} %pad_maximum_fusion.3.m0), channel_id=1, source_target_pairs={{0,3},{1,2},{2,1},{3,0},{4,7},{5,6},{6,5},{7,4},{8,11},{9,10},{10,... | collective-permute-start | bytes 29192 | tf_op jit(solution)/shard_map/ppermute | solution.py:168
  10.2 2.1 %collective-permute-done.1.m1 = f32[19,128]{1,0:T(8,128)S(1)} collective-permute-done((f32[19,128]{1,0:T(8,128)S(1)}, f32[19,128]{1,0:T(8,128)S(1)}, u32[]{:S(2)}, u32[]{:S(2)}) %collective-permute-start.1) | collective-permute-done | bytes 9760 | tf_op jit(solution)/shard_map/ppermute | solution.py:168
  12.3 1.3 %shard_map.76 = (bf16[704,512]{1,0:T(8,128)(2,1)}, bf16[704,512]{1,0:T(8,128)(2,1)}, f32[11,128]{1,0:T(8,128)S(1)}) custom-call(f32[1408,512]{1,0:T(8,128)S(1)} %get-tuple-element.12.fresh_ref, f32[19,128]{1,0:T(8,128)S(1)} %pad_maximum_fusion.3.m0, f32[19,128]{1,0:T(8,128)S(1)} %collective-permute-done.1.m1), custom_call_target="tpu_custom_call" | custom-call | tf_op jit(solution)/shard_map/pallas_call | solution.py:30
  13.7 0.3 collective-permute-start.2
  13.9 3.0 %collective-permute-start.4 = (bf16[704,512]{1,0:T(8,128)(2,1)}, bf16[704,512]{1,0:T(8,128)(2,1)}, u32[]{:S(2)}, u32[]{:S(2)}) collective-permute-start(bf16[704,512]{1,0:T(8,128)(2,1)} %get-tuple-element.15.b_ref), channel_id=1, source_target_pairs={{0,3},{1,0},{2,1},{3,2},{4,7},{5,4},{6,5},{7,6},{8,11},{9,8},{10,9... | collective-permute-start | bytes 2162696 | tf_op jit(solution)/shard_map/ppermute | solution.py:168
  16.9 0.1 collective-permute-start.8
  17.0 1.2 %collective-permute-done.8 = f32[16,128]{1,0:T(8,128)S(1)} collective-permute-done((f32[16,128]{1,0:T(8,128)S(1)}, f32[16,128]{1,0:T(8,128)S(1)}, u32[]{:S(2)}, u32[]{:S(2)}) %collective-permute-start.8) | collective-permute-done | bytes 8224 | tf_op jit(solution)/shard_map/ppermute | solution.py:168
  18.2 0.8 %collective-permute-start.9 = (f32[32,128]{1,0:T(8,128)S(1)}, f32[32,128]{1,0:T(8,128)S(1)}, u32[]{:S(2)}, u32[]{:S(2)}) collective-permute-start(f32[32,128]{1,0:T(8,128)S(1)} %pad_maximum_fusion.2), channel_id=1, source_target_pairs={{0,8},{4,12},{8,0},{12,4},{16,24},{20,28},{24,16},{28,20},{32,40},... | collective-permute-start | bytes 49160 | tf_op jit(solution)/shard_map/ppermute | solution.py:168
  19.0 3.2 %collective-permute-start.7 = (bf16[704,512]{1,0:T(8,128)(2,1)}, bf16[704,512]{1,0:T(8,128)(2,1)}, u32[]{:S(2)}, u32[]{:S(2)}) collective-permute-start(bf16[704,512]{1,0:T(8,128)(2,1)} %get-tuple-element.14.a_ref), channel_id=1, source_target_pairs={{0,3},{1,0},{2,1},{3,2},{4,7},{5,4},{6,5},{7,6},{8,11},{9,8},{10,9... | collective-permute-start | bytes 2162696 | tf_op jit(solution)/shard_map/ppermute | solution.py:168
  22.2 12.0 %collective-permute-done.2.refs_0_ = bf16[704,512]{1,0:T(8,128)(2,1)} collective-permute-done((bf16[704,512]{1,0:T(8,128)(2,1)}, bf16[704,512]{1,0:T(8,128)(2,1)}, u32[]{:S(2)}, u32[]{:S(2)}) %collective-permute-start.2) | collective-permute-done | bytes 720928 | tf_op jit(solution)/shard_map/ppermute | solution.py:168
  34.2 0.0 collective-permute-start.3
  34.2 0.0 collective-permute-done.4.refs_1_
  34.2 3.2 %collective-permute-start.5 = (bf16[704,512]{1,0:T(8,128)(2,1)}, bf16[704,512]{1,0:T(8,128)(2,1)}, u32[]{:S(2)}, u32[]{:S(2)}) collective-permute-start(bf16[704,512]{1,0:T(8,128)(2,1)} %collective-permute-done.4.refs_1_), channel_id=1, source_target_pairs={{0,3},{1,0},{2,1},{3,2},{4,7},{5,4},{6,5},{7,6},{8,11},{9,8},{10,9... | collective-permute-start | bytes 2162696 | tf_op jit(solution)/shard_map/ppermute | solution.py:168
  37.4 0.0 collective-permute-done.9
  37.5 2.0 %collective-permute-start.10 = (f32[64,128]{1,0:T(8,128)S(1)}, f32[64,128]{1,0:T(8,128)S(1)}, u32[]{:S(2)}, u32[]{:S(2)}) collective-permute-start(f32[64,128]{1,0:T(8,128)S(1)} %concatenate.33), channel_id=1, source_target_pairs={{0,24},{4,28},{8,16},{12,20},{16,8},{20,12},{24,0},{28,4},{32,56},... | collective-permute-start | bytes 98312 | tf_op jit(solution)/shard_map/ppermute | solution.py:168
  39.5 3.2 %collective-permute-done.10 = f32[64,128]{1,0:T(8,128)S(1)} collective-permute-done((f32[64,128]{1,0:T(8,128)S(1)}, f32[64,128]{1,0:T(8,128)S(1)}, u32[]{:S(2)}, u32[]{:S(2)}) %collective-permute-start.10) | collective-permute-done | bytes 32800 | tf_op jit(solution)/shard_map/ppermute | solution.py:168
  42.7 0.1 shard_map.81
  42.8 2.0 %collective-permute-start.11 = (bf16[8,2048]{1,0:T(8,128)(2,1)S(1)}, bf16[8,2048]{1,0:T(8,128)(2,1)S(1)}, u32[]{:S(2)}, u32[]{:S(2)}) collective-permute-start(bf16[8,2048]{1,0:T(8,128)(2,1)S(1)} %shard_map.81), channel_id=1, source_target_pairs={{0,32},{4,36},{8,40},{12,44},{16,48},{20,52},{24,56},{28,60},{32,0... | collective-permute-start | bytes 98312 | tf_op jit(solution)/shard_map/ppermute | solution.py:168
  44.8 2.0 %collective-permute-done.11 = bf16[8,2048]{1,0:T(8,128)(2,1)S(1)} collective-permute-done((bf16[8,2048]{1,0:T(8,128)(2,1)S(1)}, bf16[8,2048]{1,0:T(8,128)(2,1)S(1)}, u32[]{:S(2)}, u32[]{:S(2)}) %collective-permute-start.11) | collective-permute-done | bytes 32800 | tf_op jit(solution)/shard_map/ppermute | solution.py:168
  46.8 3.3 %collective-permute-start.12 = (bf16[16,2048]{1,0:T(8,128)(2,1)S(1)}, bf16[16,2048]{1,0:T(8,128)(2,1)S(1)}, u32[]{:S(2)}, u32[]{:S(2)}) collective-permute-start(bf16[16,2048]{1,0:T(8,128)(2,1)S(1)} %pad_maximum_fusion.1), channel_id=1, source_target_pairs={{0,64},{4,68},{8,72},{12,76},{16,80},{20,84},{24,88},{28,92},{32,9... | collective-permute-start | bytes 196616 | tf_op jit(solution)/shard_map/ppermute | solution.py:168
  50.0 2.3 %collective-permute-done.12 = bf16[16,2048]{1,0:T(8,128)(2,1)S(1)} collective-permute-done((bf16[16,2048]{1,0:T(8,128)(2,1)S(1)}, bf16[16,2048]{1,0:T(8,128)(2,1)S(1)}, u32[]{:S(2)}, u32[]{:S(2)}) %collective-permute-start.12) | collective-permute-done | bytes 65568 | tf_op jit(solution)/shard_map/ppermute | solution.py:168
  52.4 6.2 %collective-permute-start.13 = (bf16[32,2048]{1,0:T(8,128)(2,1)S(1)}, bf16[32,2048]{1,0:T(8,128)(2,1)S(1)}, u32[]{:S(2)}, u32[]{:S(2)}) collective-permute-start(bf16[32,2048]{1,0:T(8,128)(2,1)S(1)} %pad_maximum_fusion.refs_0_), channel_id=1, source_target_pairs={{0,224},{4,228},{8,232},{12,236},{16,240},{20,244},{24,248},{28,25... | collective-permute-start | bytes 393224 | tf_op jit(solution)/shard_map/ppermute | solution.py:168
  58.6 3.4 %shard_map.77 = (bf16[1,1408,2048]{2,1,0:T(8,128)(2,1)}, f32[1,1408,512]{2,1,0:T(8,128)}, f32[1,1408]{1,0:T(1,128)}) custom-call(bf16[704,512]{1,0:T(8,128)(2,1)} %get-tuple-element.14.a_ref, bf16[704,512]{1,0:T(8,128)(2,1)} %get-tuple-element.15.b_ref, f32[1408,512]{1,0:T(8,128)S(1)} %get-tuple-element.12.fresh_ref, f32[11,128]{1,0:T(8,128)S(1)} %get-tuple-element.16.scale_ref), custom_call_target="tpu_custom_call" | custom-call | tf_op jit(solution)/shard_map/pallas_call | solution.py:30
  62.0 0.8 %collective-permute-done.13.refs_1_ = bf16[32,2048]{1,0:T(8,128)(2,1)S(1)} collective-permute-done((bf16[32,2048]{1,0:T(8,128)(2,1)S(1)}, bf16[32,2048]{1,0:T(8,128)(2,1)S(1)}, u32[]{:S(2)}, u32[]{:S(2)}) %collective-permute-start.13) | collective-permute-done | bytes 131104 | tf_op jit(solution)/shard_map/ppermute | solution.py:168
  62.8 0.8 %shard_map.82 = bf16[64,2048]{1,0:T(8,128)(2,1)} custom-call(bf16[32,2048]{1,0:T(8,128)(2,1)S(1)} %pad_maximum_fusion.refs_0_, bf16[32,2048]{1,0:T(8,128)(2,1)S(1)} %collective-permute-done.13.refs_1_), custom_call_target="tpu_custom_call" | custom-call | tf_op jit(solution)/shard_map/pallas_call | solution.py:30
  63.6 2.4 %shard_map.78.refs_2_ = bf16[1,1408,2048]{2,1,0:T(8,128)(2,1)} custom-call(bf16[704,512]{1,0:T(8,128)(2,1)} %collective-permute-done.2.refs_0_, bf16[704,512]{1,0:T(8,128)(2,1)} %collective-permute-done.4.refs_1_, bf16[1,1408,2048]{2,1,0:T(8,128)(2,1)} %get-tuple-element.17.refs_2_), custom_call_target="tpu_custom_call", output_to_operand_aliasing={{}: (2, {})} | custom-call | tf_op jit(solution)/shard_map/pallas_call | solution.py:30
  66.0 0.0 collective-permute-done.6.refs_0_
  66.0 2.4 %shard_map.79.refs_2_ = bf16[1,1408,2048]{2,1,0:T(8,128)(2,1)} custom-call(bf16[704,512]{1,0:T(8,128)(2,1)} %collective-permute-done.6.refs_0_, bf16[704,512]{1,0:T(8,128)(2,1)} %collective-permute-done.7.refs_1_, bf16[1,1408,2048]{2,1,0:T(8,128)(2,1)} %shard_map.78.refs_2_), custom_call_target="tpu_custom_call", output_to_operand_aliasing={{}: (2, {})} | custom-call | tf_op jit(solution)/shard_map/pallas_call | solution.py:30
  68.5 2.4 %shard_map.80 = bf16[1,1408,2048]{2,1,0:T(8,128)(2,1)} custom-call(bf16[704,512]{1,0:T(8,128)(2,1)} %collective-permute-done.3.refs_0_, bf16[704,512]{1,0:T(8,128)(2,1)} %collective-permute-done.5.refs_1_, bf16[1,1408,2048]{2,1,0:T(8,128)(2,1)} %shard_map.79.refs_2_), custom_call_target="tpu_custom_call", output_to_operand_aliasing={{}: (2, {})} | custom-call | tf_op jit(solution)/shard_map/pallas_call | solution.py:30
  (15 shorter events, 0.1 us)
Async XLA Ops:
  3.6 3.7 %collective-permute-start = (f32[15,128]{1,0:T(8,128)S(1)}, f32[15,128]{1,0:T(8,128)S(1)}, u32[]{:S(2)}, u32[]{:S(2)}) collective-permute-start(f32[15,128]{1,0:T(8,128)S(1)} %get-tuple-element.13), channel_id=1, source_target_pairs={{0,1},{1,0},{2,3},{3,2},{4,5},{5,4},{6,7},{7,6},{8,9},{9,8},{10,11... | collective-permute-start | bytes 23048 | tf_op jit(solution)/shard_map/ppermute | solution.py:168
  7.3 5.0 %collective-permute-start.1 = (f32[19,128]{1,0:T(8,128)S(1)}, f32[19,128]{1,0:T(8,128)S(1)}, u32[]{:S(2)}, u32[]{:S(2)}) collective-permute-start(f32[19,128]{1,0:T(8,128)S(1)} %pad_maximum_fusion.3.m0), channel_id=1, source_target_pairs={{0,3},{1,2},{2,1},{3,0},{4,7},{5,6},{6,5},{7,4},{8,11},{9,10},{10,... | collective-permute-start | bytes 29192 | tf_op jit(solution)/shard_map/ppermute | solution.py:168
  13.7 20.5 %collective-permute-start.2 = (bf16[704,512]{1,0:T(8,128)(2,1)}, bf16[704,512]{1,0:T(8,128)(2,1)}, u32[]{:S(2)}, u32[]{:S(2)}) collective-permute-start(bf16[704,512]{1,0:T(8,128)(2,1)} %get-tuple-element.14.a_ref), channel_id=1, source_target_pairs={{0,1},{1,2},{2,3},{3,0},{4,5},{5,6},{6,7},{7,4},{8,9},{9,10},{10,1... | collective-permute-start | bytes 2162696 | tf_op jit(solution)/shard_map/ppermute | solution.py:168
  13.9 20.3 %collective-permute-start.4 = (bf16[704,512]{1,0:T(8,128)(2,1)}, bf16[704,512]{1,0:T(8,128)(2,1)}, u32[]{:S(2)}, u32[]{:S(2)}) collective-permute-start(bf16[704,512]{1,0:T(8,128)(2,1)} %get-tuple-element.15.b_ref), channel_id=1, source_target_pairs={{0,3},{1,0},{2,1},{3,2},{4,7},{5,4},{6,5},{7,6},{8,11},{9,8},{10,9... | collective-permute-start | bytes 2162696 | tf_op jit(solution)/shard_map/ppermute | solution.py:168
  16.9 1.3 %collective-permute-start.8 = (f32[16,128]{1,0:T(8,128)S(1)}, f32[16,128]{1,0:T(8,128)S(1)}, u32[]{:S(2)}, u32[]{:S(2)}) collective-permute-start(f32[16,128]{1,0:T(8,128)S(1)} %pad_maximum_fusion.4), channel_id=1, source_target_pairs={{0,4},{4,0},{8,12},{12,8},{16,20},{20,16},{24,28},{28,24},{32,36},... | collective-permute-start | bytes 24584 | tf_op jit(solution)/shard_map/ppermute | solution.py:168
  18.2 19.3 %collective-permute-start.9 = (f32[32,128]{1,0:T(8,128)S(1)}, f32[32,128]{1,0:T(8,128)S(1)}, u32[]{:S(2)}, u32[]{:S(2)}) collective-permute-start(f32[32,128]{1,0:T(8,128)S(1)} %pad_maximum_fusion.2), channel_id=1, source_target_pairs={{0,8},{4,12},{8,0},{12,4},{16,24},{20,28},{24,16},{28,20},{32,40},... | collective-permute-start | bytes 49160 | tf_op jit(solution)/shard_map/ppermute | solution.py:168
  19.0 47.0 %collective-permute-start.6 = (bf16[704,512]{1,0:T(8,128)(2,1)}, bf16[704,512]{1,0:T(8,128)(2,1)}, u32[]{:S(2)}, u32[]{:S(2)}) collective-permute-start(bf16[704,512]{1,0:T(8,128)(2,1)} %get-tuple-element.15.b_ref), channel_id=1, source_target_pairs={{0,1},{1,2},{2,3},{3,0},{4,5},{5,6},{6,7},{7,4},{8,9},{9,10},{10,1... | collective-permute-start | bytes 2162696 | tf_op jit(solution)/shard_map/ppermute | solution.py:168
  19.0 47.0 %collective-permute-start.7 = (bf16[704,512]{1,0:T(8,128)(2,1)}, bf16[704,512]{1,0:T(8,128)(2,1)}, u32[]{:S(2)}, u32[]{:S(2)}) collective-permute-start(bf16[704,512]{1,0:T(8,128)(2,1)} %get-tuple-element.14.a_ref), channel_id=1, source_target_pairs={{0,3},{1,0},{2,1},{3,2},{4,7},{5,4},{6,5},{7,6},{8,11},{9,8},{10,9... | collective-permute-start | bytes 2162696 | tf_op jit(solution)/shard_map/ppermute | solution.py:168
  34.2 34.3 %collective-permute-start.3 = (bf16[704,512]{1,0:T(8,128)(2,1)}, bf16[704,512]{1,0:T(8,128)(2,1)}, u32[]{:S(2)}, u32[]{:S(2)}) collective-permute-start(bf16[704,512]{1,0:T(8,128)(2,1)} %collective-permute-done.2.refs_0_), channel_id=1, source_target_pairs={{0,1},{1,2},{2,3},{3,0},{4,5},{5,6},{6,7},{7,4},{8,9},{9,10},{10,1... | collective-permute-start | bytes 2162696 | tf_op jit(solution)/shard_map/ppermute | solution.py:168
  34.2 34.3 %collective-permute-start.5 = (bf16[704,512]{1,0:T(8,128)(2,1)}, bf16[704,512]{1,0:T(8,128)(2,1)}, u32[]{:S(2)}, u32[]{:S(2)}) collective-permute-start(bf16[704,512]{1,0:T(8,128)(2,1)} %collective-permute-done.4.refs_1_), channel_id=1, source_target_pairs={{0,3},{1,0},{2,1},{3,2},{4,7},{5,4},{6,5},{7,6},{8,11},{9,8},{10,9... | collective-permute-start | bytes 2162696 | tf_op jit(solution)/shard_map/ppermute | solution.py:168
  37.5 5.2 %collective-permute-start.10 = (f32[64,128]{1,0:T(8,128)S(1)}, f32[64,128]{1,0:T(8,128)S(1)}, u32[]{:S(2)}, u32[]{:S(2)}) collective-permute-start(f32[64,128]{1,0:T(8,128)S(1)} %concatenate.33), channel_id=1, source_target_pairs={{0,24},{4,28},{8,16},{12,20},{16,8},{20,12},{24,0},{28,4},{32,56},... | collective-permute-start | bytes 98312 | tf_op jit(solution)/shard_map/ppermute | solution.py:168
  42.8 4.0 %collective-permute-start.11 = (bf16[8,2048]{1,0:T(8,128)(2,1)S(1)}, bf16[8,2048]{1,0:T(8,128)(2,1)S(1)}, u32[]{:S(2)}, u32[]{:S(2)}) collective-permute-start(bf16[8,2048]{1,0:T(8,128)(2,1)S(1)} %shard_map.81), channel_id=1, source_target_pairs={{0,32},{4,36},{8,40},{12,44},{16,48},{20,52},{24,56},{28,60},{32,0... | collective-permute-start | bytes 98312 | tf_op jit(solution)/shard_map/ppermute | solution.py:168
  46.8 5.6 %collective-permute-start.12 = (bf16[16,2048]{1,0:T(8,128)(2,1)S(1)}, bf16[16,2048]{1,0:T(8,128)(2,1)S(1)}, u32[]{:S(2)}, u32[]{:S(2)}) collective-permute-start(bf16[16,2048]{1,0:T(8,128)(2,1)S(1)} %pad_maximum_fusion.1), channel_id=1, source_target_pairs={{0,64},{4,68},{8,72},{12,76},{16,80},{20,84},{24,88},{28,92},{32,9... | collective-permute-start | bytes 196616 | tf_op jit(solution)/shard_map/ppermute | solution.py:168
  52.4 10.4 %collective-permute-start.13 = (bf16[32,2048]{1,0:T(8,128)(2,1)S(1)}, bf16[32,2048]{1,0:T(8,128)(2,1)S(1)}, u32[]{:S(2)}, u32[]{:S(2)}) collective-permute-start(bf16[32,2048]{1,0:T(8,128)(2,1)S(1)} %pad_maximum_fusion.refs_0_), channel_id=1, source_target_pairs={{0,224},{4,228},{8,232},{12,236},{16,240},{20,244},{24,248},{28,25... | collective-permute-start | bytes 393224 | tf_op jit(solution)/shard_map/ppermute | solution.py:168

commit v2 on v1

--- a/solution.py
+++ b/solution.py
@@ -34,8 +34,16 @@
         out_specs=out_specs,
         scratch_shapes=list(scratch),
         input_output_aliases=aliases or {},
-        compiler_params=pltpu.CompilerParams(vmem_limit_bytes=40 * 1024 * 1024),
+        compiler_params=pltpu.CompilerParams(vmem_limit_bytes=12 * 1024 * 1024),
     )(*ins)
+
+
+def stacked(one, two):
+    low = jnp.array(-jnp.inf, one.dtype)
+    return jnp.maximum(
+        lax.pad(one, low, ((0, two.shape[0], 0), (0, 0, 0))),
+        lax.pad(two, low, ((one.shape[0], 0, 0), (0, 0, 0))),
+    )
 
 
 def run(copies):
@@ -171,7 +179,7 @@
         return move(v, "fsdp", lambda i: (i + by) % xs)
 
     def swap(v, step):
-        return jnp.concatenate([v, move(v, "ep", lambda e: e ^ step)], 0)
+        return stacked(v, move(v, "ep", lambda e: e ^ step))
 
     fresh, msg = call(
         functools.partial(fresh_kernel, groups),
@@ -206,7 +214,7 @@
     out = place(out, [b_r, a_l], [(1, half), (3, 0)])
     out = place(out, [a_rr, b_ll], [(2, 0), (2, half)])
 
-    lines = jnp.concatenate([msg[groups:], other[groups:]], 0)
+    lines = stacked(msg[groups:], other[groups:])
     lines = swap(lines, 1)
     lines = swap(lines, CORES)
     lines = swap(lines, CORES * 3)
@@ -216,9 +224,9 @@
         pltpu.VMEM((per, cols * xs), BF16), VM, [pltpu.VMEM((per * xs * part, LANES), F32)],
     )
     two = move(block, "ep", lambda e: e ^ per)
-    both = jnp.concatenate([block, two], 0)
+    both = stacked(block, two)
     four = move(both, "ep", lambda e: e ^ (per * 2))
-    both = jnp.concatenate([both, four], 0)
+    both = stacked(both, four)
     eight = move(both, "ep", lambda e: e ^ (per * 7))
     router = call(
         router_place_kernel,

time: 71.1 us -> 61.8 us (0.87)
  the two profiles are of different devices: /device:TPU:24 before, /device:TPU:134 now
where the time goes in v2:
time: 61.8 us; the launch traced here: 61.7 us
  waiting for transfers between devices  36.4 us (59%)
  starting transfers between devices  15 us (24%)
  Pallas kernels  9.56 us (15%)
  between operations  0.74 us (1%)
    ppermute x14, waiting for transfers between devices, move(): lax.ppermute(v, axis, [(i, to(i)) for i in range(lax.axis_size(axis))])  36.4 us
    ppermute x14, starting transfers between devices, move(): lax.ppermute(v, axis, [(i, to(i)) for i in range(lax.axis_size(axis))])  15 us
    pallas_call x8, Pallas kernels, call(): pl.pallas_call(kernel, out_shape=outs, in_specs=in_specs, out_specs=out_s...  9.56 us
  transfers between devices with their start and end apart: 14, of which 10 were waited for; matrix products, arithmetic and copies ran while one was open for 0% of the time, Pallas kernels for 8%

profile of v2, /device:TPU:134, one launch (start us, length us, event | category | flops | bytes accessed | tf_op | source)
XLA Modules:
  0.0 61.7 jit_solution(12293864365368471637)
XLA Ops:
  0.6 3.0 %shard_map.75 = (f32[1408,512]{1,0:T(8,128)S(1)}, f32[15,128]{1,0:T(8,128)S(1)}) custom-call(f32[1,1408,512]{2,1,0:T(8,128)} %w_hbm.1, f32[1,1408,512]{2,1,0:T(8,128)} %a_hbm.1, f32[1,512]{1,0:T(1,128)} %bitcast.4, f32[1,512]{1,0:T(1,128)} %bitcast.5), custom_call_target="tpu_custom_call" | custom-call | tf_op jit(solution)/shard_map/pallas_call | solution.py:30
  3.6 0.9 %collective-permute-start = (f32[15,128]{1,0:T(8,128)S(1)}, f32[15,128]{1,0:T(8,128)S(1)}, u32[]{:S(2)}, u32[]{:S(2)}) collective-permute-start(f32[15,128]{1,0:T(8,128)S(1)} %get-tuple-element.13), channel_id=1, source_target_pairs={{0,1},{1,0},{2,3},{3,2},{4,5},{5,4},{6,7},{7,6},{8,9},{9,8},{10,11... | collective-permute-start | bytes 23048 | tf_op jit(solution)/shard_map/ppermute | solution.py:176
  4.5 2.8 %collective-permute-done = f32[15,128]{1,0:T(8,128)S(1)} collective-permute-done((f32[15,128]{1,0:T(8,128)S(1)}, f32[15,128]{1,0:T(8,128)S(1)}, u32[]{:S(2)}, u32[]{:S(2)}) %collective-permute-start) | collective-permute-done | bytes 7712 | tf_op jit(solution)/shard_map/ppermute | solution.py:176
  7.3 0.6 collective-permute-start.1
  7.9 4.4 %collective-permute-done.1.m1 = f32[19,128]{1,0:T(8,128)S(1)} collective-permute-done((f32[19,128]{1,0:T(8,128)S(1)}, f32[19,128]{1,0:T(8,128)S(1)}, u32[]{:S(2)}, u32[]{:S(2)}) %collective-permute-start.1) | collective-permute-done | bytes 9760 | tf_op jit(solution)/shard_map/ppermute | solution.py:176
  12.3 0.3 shard_map.76
  12.7 0.6 collective-permute-start.2
  13.2 1.5 %collective-permute-start.4 = (bf16[704,512]{1,0:T(8,128)(2,1)S(1)}, bf16[704,512]{1,0:T(8,128)(2,1)S(1)}, u32[]{:S(2)}, u32[]{:S(2)}) collective-permute-start(bf16[704,512]{1,0:T(8,128)(2,1)S(1)} %get-tuple-element.15.b_ref), channel_id=1, source_target_pairs={{0,3},{1,0},{2,1},{3,2},{4,7},{5,4},{6,5},{7,6},{8,11},{9,8},{10,9... | collective-permute-start | bytes 2162696 | tf_op jit(solution)/shard_map/ppermute | solution.py:176
  14.8 0.1 collective-permute-start.8
  14.9 1.2 %collective-permute-done.8 = f32[16,128]{1,0:T(8,128)S(1)} collective-permute-done((f32[16,128]{1,0:T(8,128)S(1)}, f32[16,128]{1,0:T(8,128)S(1)}, u32[]{:S(2)}, u32[]{:S(2)}) %collective-permute-start.8) | collective-permute-done | bytes 8224 | tf_op jit(solution)/shard_map/ppermute | solution.py:176
  16.0 1.6 %collective-permute-start.9 = (f32[32,128]{1,0:T(8,128)S(1)}, f32[32,128]{1,0:T(8,128)S(1)}, u32[]{:S(2)}, u32[]{:S(2)}) collective-permute-start(f32[32,128]{1,0:T(8,128)S(1)} %pad_maximum_fusion.4), channel_id=1, source_target_pairs={{0,8},{4,12},{8,0},{12,4},{16,24},{20,28},{24,16},{28,20},{32,40},... | collective-permute-start | bytes 49160 | tf_op jit(solution)/shard_map/ppermute | solution.py:176
  17.6 2.2 %collective-permute-done.9 = f32[32,128]{1,0:T(8,128)S(1)} collective-permute-done((f32[32,128]{1,0:T(8,128)S(1)}, f32[32,128]{1,0:T(8,128)S(1)}, u32[]{:S(2)}, u32[]{:S(2)}) %collective-permute-start.9) | collective-permute-done | bytes 16416 | tf_op jit(solution)/shard_map/ppermute | solution.py:176
  19.8 3.0 %collective-permute-start.10 = (f32[64,128]{1,0:T(8,128)S(1)}, f32[64,128]{1,0:T(8,128)S(1)}, u32[]{:S(2)}, u32[]{:S(2)}) collective-permute-start(f32[64,128]{1,0:T(8,128)S(1)} %pad_maximum_fusion.3), channel_id=1, source_target_pairs={{0,24},{4,28},{8,16},{12,20},{16,8},{20,12},{24,0},{28,4},{32,56},... | collective-permute-start | bytes 98312 | tf_op jit(solution)/shard_map/ppermute | solution.py:176
  22.8 1.7 %collective-permute-start.6 = (bf16[704,512]{1,0:T(8,128)(2,1)S(1)}, bf16[704,512]{1,0:T(8,128)(2,1)S(1)}, u32[]{:S(2)}, u32[]{:S(2)}) collective-permute-start(bf16[704,512]{1,0:T(8,128)(2,1)S(1)} %get-tuple-element.15.b_ref), channel_id=1, source_target_pairs={{0,1},{1,2},{2,3},{3,0},{4,5},{5,6},{6,7},{7,4},{8,9},{9,10},{10,1... | collective-permute-start | bytes 2162696 | tf_op jit(solution)/shard_map/ppermute | solution.py:176
  24.5 0.3 collective-permute-start.7
  24.8 6.9 %collective-permute-done.2.refs_0_ = bf16[704,512]{1,0:T(8,128)(2,1)S(1)} collective-permute-done((bf16[704,512]{1,0:T(8,128)(2,1)S(1)}, bf16[704,512]{1,0:T(8,128)(2,1)S(1)}, u32[]{:S(2)}, u32[]{:S(2)}) %collective-permute-start.2) | collective-permute-done | bytes 720928 | tf_op jit(solution)/shard_map/ppermute | solution.py:176
  31.7 0.9 %collective-permute-start.3 = (bf16[704,512]{1,0:T(8,128)(2,1)S(1)}, bf16[704,512]{1,0:T(8,128)(2,1)S(1)}, u32[]{:S(2)}, u32[]{:S(2)}) collective-permute-start(bf16[704,512]{1,0:T(8,128)(2,1)S(1)} %collective-permute-done.2.refs_0_), channel_id=1, source_target_pairs={{0,1},{1,2},{2,3},{3,0},{4,5},{5,6},{6,7},{7,4},{8,9},{9,10},{10,1... | collective-permute-start | bytes 2162696 | tf_op jit(solution)/shard_map/ppermute | solution.py:176
  32.7 1.1 %collective-permute-start.5 = (bf16[704,512]{1,0:T(8,128)(2,1)S(1)}, bf16[704,512]{1,0:T(8,128)(2,1)S(1)}, u32[]{:S(2)}, u32[]{:S(2)}) collective-permute-start(bf16[704,512]{1,0:T(8,128)(2,1)S(1)} %collective-permute-done.4.refs_1_), channel_id=1, source_target_pairs={{0,3},{1,0},{2,1},{3,2},{4,7},{5,4},{6,5},{7,6},{8,11},{9,8},{10,9... | collective-permute-start | bytes 2162696 | tf_op jit(solution)/shard_map/ppermute | solution.py:176
  33.8 0.1 shard_map.81
  33.9 1.1 %collective-permute-start.11 = (bf16[8,2048]{1,0:T(8,128)(2,1)S(1)}, bf16[8,2048]{1,0:T(8,128)(2,1)S(1)}, u32[]{:S(2)}, u32[]{:S(2)}) collective-permute-start(bf16[8,2048]{1,0:T(8,128)(2,1)S(1)} %shard_map.81), channel_id=1, source_target_pairs={{0,32},{4,36},{8,40},{12,44},{16,48},{20,52},{24,56},{28,60},{32,0... | collective-permute-start | bytes 98312 | tf_op jit(solution)/shard_map/ppermute | solution.py:176
  35.0 2.9 %collective-permute-done.11 = bf16[8,2048]{1,0:T(8,128)(2,1)S(1)} collective-permute-done((bf16[8,2048]{1,0:T(8,128)(2,1)S(1)}, bf16[8,2048]{1,0:T(8,128)(2,1)S(1)}, u32[]{:S(2)}, u32[]{:S(2)}) %collective-permute-start.11) | collective-permute-done | bytes 32800 | tf_op jit(solution)/shard_map/ppermute | solution.py:176
  37.9 1.5 %collective-permute-start.12 = (bf16[16,2048]{1,0:T(8,128)(2,1)S(1)}, bf16[16,2048]{1,0:T(8,128)(2,1)S(1)}, u32[]{:S(2)}, u32[]{:S(2)}) collective-permute-start(bf16[16,2048]{1,0:T(8,128)(2,1)S(1)} %pad_maximum_fusion.1), channel_id=1, source_target_pairs={{0,64},{4,68},{8,72},{12,76},{16,80},{20,84},{24,88},{28,92},{32,9... | collective-permute-start | bytes 196616 | tf_op jit(solution)/shard_map/ppermute | solution.py:176
  39.3 4.4 %collective-permute-done.12 = bf16[16,2048]{1,0:T(8,128)(2,1)S(1)} collective-permute-done((bf16[16,2048]{1,0:T(8,128)(2,1)S(1)}, bf16[16,2048]{1,0:T(8,128)(2,1)S(1)}, u32[]{:S(2)}, u32[]{:S(2)}) %collective-permute-start.12) | collective-permute-done | bytes 65568 | tf_op jit(solution)/shard_map/ppermute | solution.py:176
  43.8 0.1 collective-permute-start.13
  43.9 2.1 %shard_map.77 = (bf16[1,1408,2048]{2,1,0:T(8,128)(2,1)}, f32[1,1408,512]{2,1,0:T(8,128)}, f32[1,1408]{1,0:T(1,128)}) custom-call(bf16[704,512]{1,0:T(8,128)(2,1)S(1)} %get-tuple-element.14.a_ref, bf16[704,512]{1,0:T(8,128)(2,1)S(1)} %get-tuple-element.15.b_ref, f32[1408,512]{1,0:T(8,128)S(1)} %get-tuple-element.12.fresh_ref, ...), custom_call_target="tpu_custom_call" | custom-call | tf_op jit(solution)/shard_map/pallas_call | solution.py:30
  46.0 5.5 %collective-permute-done.13.refs_1_ = bf16[32,2048]{1,0:T(8,128)(2,1)S(1)} collective-permute-done((bf16[32,2048]{1,0:T(8,128)(2,1)S(1)}, bf16[32,2048]{1,0:T(8,128)(2,1)S(1)}, u32[]{:S(2)}, u32[]{:S(2)}) %collective-permute-start.13) | collective-permute-done | bytes 131104 | tf_op jit(solution)/shard_map/ppermute | solution.py:176
  51.4 0.8 %shard_map.82 = bf16[64,2048]{1,0:T(8,128)(2,1)} custom-call(bf16[32,2048]{1,0:T(8,128)(2,1)S(1)} %pad_maximum_fusion.refs_0_, bf16[32,2048]{1,0:T(8,128)(2,1)S(1)} %collective-permute-done.13.refs_1_), custom_call_target="tpu_custom_call" | custom-call | tf_op jit(solution)/shard_map/pallas_call | solution.py:30
  52.2 1.1 %shard_map.78.refs_2_ = bf16[1,1408,2048]{2,1,0:T(8,128)(2,1)} custom-call(bf16[704,512]{1,0:T(8,128)(2,1)S(1)} %collective-permute-done.2.refs_0_, bf16[704,512]{1,0:T(8,128)(2,1)S(1)} %collective-permute-done.4.refs_1_, bf16[1,1408,2048]{2,1,0:T(8,128)(2,1)} %get-tuple-element.17.refs_2_), custom_call_target="tpu_custom_call", output_to_operand_aliasing={{}: (2, {})} | custom-call | tf_op jit(solution)/shard_map/pallas_call | solution.py:30
  53.4 1.1 %shard_map.79.refs_2_ = bf16[1,1408,2048]{2,1,0:T(8,128)(2,1)} custom-call(bf16[704,512]{1,0:T(8,128)(2,1)S(1)} %collective-permute-done.6.refs_0_, bf16[704,512]{1,0:T(8,128)(2,1)S(1)} %collective-permute-done.7.refs_1_, bf16[1,1408,2048]{2,1,0:T(8,128)(2,1)} %shard_map.78.refs_2_), custom_call_target="tpu_custom_call", output_to_operand_aliasing={{}: (2, {})} | custom-call | tf_op jit(solution)/shard_map/pallas_call | solution.py:30
  54.5 4.7 %collective-permute-done.3.refs_0_ = bf16[704,512]{1,0:T(8,128)(2,1)S(1)} collective-permute-done((bf16[704,512]{1,0:T(8,128)(2,1)S(1)}, bf16[704,512]{1,0:T(8,128)(2,1)S(1)}, u32[]{:S(2)}, u32[]{:S(2)}) %collective-permute-start.3) | collective-permute-done | bytes 720928 | tf_op jit(solution)/shard_map/ppermute | solution.py:176
  59.2 1.4 %collective-permute-done.5.refs_1_ = bf16[704,512]{1,0:T(8,128)(2,1)S(1)} collective-permute-done((bf16[704,512]{1,0:T(8,128)(2,1)S(1)}, bf16[704,512]{1,0:T(8,128)(2,1)S(1)}, u32[]{:S(2)}, u32[]{:S(2)}) %collective-permute-start.5) | collective-permute-done | bytes 720928 | tf_op jit(solution)/shard_map/ppermute | solution.py:176
  60.6 1.1 %shard_map.80 = bf16[1,1408,2048]{2,1,0:T(8,128)(2,1)} custom-call(bf16[704,512]{1,0:T(8,128)(2,1)S(1)} %collective-permute-done.3.refs_0_, bf16[704,512]{1,0:T(8,128)(2,1)S(1)} %collective-permute-done.5.refs_1_, bf16[1,1408,2048]{2,1,0:T(8,128)(2,1)} %shard_map.79.refs_2_), custom_call_target="tpu_custom_call", output_to_operand_aliasing={{}: (2, {})} | custom-call | tf_op jit(solution)/shard_map/pallas_call | solution.py:30
  (15 shorter events, 0.1 us)
Async XLA Ops:
  3.6 3.7 %collective-permute-start = (f32[15,128]{1,0:T(8,128)S(1)}, f32[15,128]{1,0:T(8,128)S(1)}, u32[]{:S(2)}, u32[]{:S(2)}) collective-permute-start(f32[15,128]{1,0:T(8,128)S(1)} %get-tuple-element.13), channel_id=1, source_target_pairs={{0,1},{1,0},{2,3},{3,2},{4,5},{5,4},{6,7},{7,6},{8,9},{9,8},{10,11... | collective-permute-start | bytes 23048 | tf_op jit(solution)/shard_map/ppermute | solution.py:176
  7.3 5.0 %collective-permute-start.1 = (f32[19,128]{1,0:T(8,128)S(1)}, f32[19,128]{1,0:T(8,128)S(1)}, u32[]{:S(2)}, u32[]{:S(2)}) collective-permute-start(f32[19,128]{1,0:T(8,128)S(1)} %pad_maximum_fusion.5.m0), channel_id=1, source_target_pairs={{0,3},{1,2},{2,1},{3,0},{4,7},{5,6},{6,5},{7,4},{8,11},{9,10},{10,... | collective-permute-start | bytes 29192 | tf_op jit(solution)/shard_map/ppermute | solution.py:176
  12.7 19.1 %collective-permute-start.2 = (bf16[704,512]{1,0:T(8,128)(2,1)S(1)}, bf16[704,512]{1,0:T(8,128)(2,1)S(1)}, u32[]{:S(2)}, u32[]{:S(2)}) collective-permute-start(bf16[704,512]{1,0:T(8,128)(2,1)S(1)} %get-tuple-element.14.a_ref), channel_id=1, source_target_pairs={{0,1},{1,2},{2,3},{3,0},{4,5},{5,6},{6,7},{7,4},{8,9},{9,10},{10,1... | collective-permute-start | bytes 2162696 | tf_op jit(solution)/shard_map/ppermute | solution.py:176
  13.2 19.5 %collective-permute-start.4 = (bf16[704,512]{1,0:T(8,128)(2,1)S(1)}, bf16[704,512]{1,0:T(8,128)(2,1)S(1)}, u32[]{:S(2)}, u32[]{:S(2)}) collective-permute-start(bf16[704,512]{1,0:T(8,128)(2,1)S(1)} %get-tuple-element.15.b_ref), channel_id=1, source_target_pairs={{0,3},{1,0},{2,1},{3,2},{4,7},{5,4},{6,5},{7,6},{8,11},{9,8},{10,9... | collective-permute-start | bytes 2162696 | tf_op jit(solution)/shard_map/ppermute | solution.py:176
  14.8 1.3 %collective-permute-start.8 = (f32[16,128]{1,0:T(8,128)S(1)}, f32[16,128]{1,0:T(8,128)S(1)}, u32[]{:S(2)}, u32[]{:S(2)}) collective-permute-start(f32[16,128]{1,0:T(8,128)S(1)} %fusion), channel_id=1, source_target_pairs={{0,4},{4,0},{8,12},{12,8},{16,20},{20,16},{24,28},{28,24},{32,36},... | collective-permute-start | bytes 24584 | tf_op jit(solution)/shard_map/ppermute | solution.py:176
  16.0 3.7 %collective-permute-start.9 = (f32[32,128]{1,0:T(8,128)S(1)}, f32[32,128]{1,0:T(8,128)S(1)}, u32[]{:S(2)}, u32[]{:S(2)}) collective-permute-start(f32[32,128]{1,0:T(8,128)S(1)} %pad_maximum_fusion.4), channel_id=1, source_target_pairs={{0,8},{4,12},{8,0},{12,4},{16,24},{20,28},{24,16},{28,20},{32,40},... | collective-permute-start | bytes 49160 | tf_op jit(solution)/shard_map/ppermute | solution.py:176
  19.8 14.0 %collective-permute-start.10 = (f32[64,128]{1,0:T(8,128)S(1)}, f32[64,128]{1,0:T(8,128)S(1)}, u32[]{:S(2)}, u32[]{:S(2)}) collective-permute-start(f32[64,128]{1,0:T(8,128)S(1)} %pad_maximum_fusion.3), channel_id=1, source_target_pairs={{0,24},{4,28},{8,16},{12,20},{16,8},{20,12},{24,0},{28,4},{32,56},... | collective-permute-start | bytes 98312 | tf_op jit(solution)/shard_map/ppermute | solution.py:176
  22.8 30.5 %collective-permute-start.6 = (bf16[704,512]{1,0:T(8,128)(2,1)S(1)}, bf16[704,512]{1,0:T(8,128)(2,1)S(1)}, u32[]{:S(2)}, u32[]{:S(2)}) collective-permute-start(bf16[704,512]{1,0:T(8,128)(2,1)S(1)} %get-tuple-element.15.b_ref), channel_id=1, source_target_pairs={{0,1},{1,2},{2,3},{3,0},{4,5},{5,6},{6,7},{7,4},{8,9},{9,10},{10,1... | collective-permute-start | bytes 2162696 | tf_op jit(solution)/shard_map/ppermute | solution.py:176
  24.5 28.9 %collective-permute-start.7 = (bf16[704,512]{1,0:T(8,128)(2,1)S(1)}, bf16[704,512]{1,0:T(8,128)(2,1)S(1)}, u32[]{:S(2)}, u32[]{:S(2)}) collective-permute-start(bf16[704,512]{1,0:T(8,128)(2,1)S(1)} %get-tuple-element.14.a_ref), channel_id=1, source_target_pairs={{0,3},{1,0},{2,1},{3,2},{4,7},{5,4},{6,5},{7,6},{8,11},{9,8},{10,9... | collective-permute-start | bytes 2162696 | tf_op jit(solution)/shard_map/ppermute | solution.py:176
  31.7 27.5 %collective-permute-start.3 = (bf16[704,512]{1,0:T(8,128)(2,1)S(1)}, bf16[704,512]{1,0:T(8,128)(2,1)S(1)}, u32[]{:S(2)}, u32[]{:S(2)}) collective-permute-start(bf16[704,512]{1,0:T(8,128)(2,1)S(1)} %collective-permute-done.2.refs_0_), channel_id=1, source_target_pairs={{0,1},{1,2},{2,3},{3,0},{4,5},{5,6},{6,7},{7,4},{8,9},{9,10},{10,1... | collective-permute-start | bytes 2162696 | tf_op jit(solution)/shard_map/ppermute | solution.py:176
  32.7 27.9 %collective-permute-start.5 = (bf16[704,512]{1,0:T(8,128)(2,1)S(1)}, bf16[704,512]{1,0:T(8,128)(2,1)S(1)}, u32[]{:S(2)}, u32[]{:S(2)}) collective-permute-start(bf16[704,512]{1,0:T(8,128)(2,1)S(1)} %collective-permute-done.4.refs_1_), channel_id=1, source_target_pairs={{0,3},{1,0},{2,1},{3,2},{4,7},{5,4},{6,5},{7,6},{8,11},{9,8},{10,9... | collective-permute-start | bytes 2162696 | tf_op jit(solution)/shard_map/ppermute | solution.py:176
  33.9 4.0 %collective-permute-start.11 = (bf16[8,2048]{1,0:T(8,128)(2,1)S(1)}, bf16[8,2048]{1,0:T(8,128)(2,1)S(1)}, u32[]{:S(2)}, u32[]{:S(2)}) collective-permute-start(bf16[8,2048]{1,0:T(8,128)(2,1)S(1)} %shard_map.81), channel_id=1, source_target_pairs={{0,32},{4,36},{8,40},{12,44},{16,48},{20,52},{24,56},{28,60},{32,0... | collective-permute-start | bytes 98312 | tf_op jit(solution)/shard_map/ppermute | solution.py:176
  37.9 5.9 %collective-permute-start.12 = (bf16[16,2048]{1,0:T(8,128)(2,1)S(1)}, bf16[16,2048]{1,0:T(8,128)(2,1)S(1)}, u32[]{:S(2)}, u32[]{:S(2)}) collective-permute-start(bf16[16,2048]{1,0:T(8,128)(2,1)S(1)} %pad_maximum_fusion.1), channel_id=1, source_target_pairs={{0,64},{4,68},{8,72},{12,76},{16,80},{20,84},{24,88},{28,92},{32,9... | collective-permute-start | bytes 196616 | tf_op jit(solution)/shard_map/ppermute | solution.py:176
  43.8 7.7 %collective-permute-start.13 = (bf16[32,2048]{1,0:T(8,128)(2,1)S(1)}, bf16[32,2048]{1,0:T(8,128)(2,1)S(1)}, u32[]{:S(2)}, u32[]{:S(2)}) collective-permute-start(bf16[32,2048]{1,0:T(8,128)(2,1)S(1)} %pad_maximum_fusion.refs_0_), channel_id=1, source_target_pairs={{0,224},{4,228},{8,232},{12,236},{16,240},{20,244},{24,248},{28,25... | collective-permute-start | bytes 393224 | tf_op jit(solution)/shard_map/ppermute | solution.py:176

commit v3 on v2

--- a/solution.py
+++ b/solution.py
@@ -53,7 +53,7 @@
         copy.wait()
 
 
-def fresh_kernel(groups, w_hbm, a_hbm, rw_hbm, rg_hbm, fresh_ref, msg_ref, w_buf, a_buf, r_buf, sems, r_sems):
+def fresh_kernel(groups, w_hbm, a_hbm, rw_hbm, rg_hbm, fresh_ref, early_ref, msg_ref, w_buf, a_buf, r_buf, sems, r_sems):
     def copies(g):
         rows = pl.ds(g * LANES, LANES)
         return (
@@ -76,6 +76,8 @@
         rows = slice(g * LANES, (g + 1) * LANES)
         fresh = 0.5 * a_buf[rows, :] + 0.5 * w_buf[rows, :]
         fresh_ref[rows, :] = fresh
+        if (g + 1) * LANES <= early_ref.shape[0]:
+            early_ref[rows, :] = fresh
         size = jnp.abs(fresh)
         top = size[:, :LANES]
         for k in range(1, size.shape[1] // LANES):
@@ -88,19 +90,38 @@
         msg_ref[groups + k : groups + k + 1, :] = part[:, k * LANES : (k + 1) * LANES]
 
 
-def serve_kernel(groups, fresh_ref, m0, m1, a_ref, b_ref, scale_ref):
-    scale_ref[...] = jnp.maximum(m0[:groups, :], m1[:groups, :])
-    rows = a_ref.shape[0]
-    for g in range(groups):
-        inverse = 1.0 / scale_ref[g : g + 1, :]
-        spread = jnp.broadcast_to(inverse, (LANES, LANES)).T
+def scaled(scale, g):
+    return jnp.broadcast_to(1.0 / scale[g : g + 1, :], (LANES, LANES)).T
+
+
+def serve_kernel(groups, fresh_ref, m0, m1, m2, m3, e_ref, a_ref, b_ref, scale_ref):
+    scale_ref[...] = jnp.maximum(
+        jnp.maximum(m0[:groups, :], m1[:groups, :]), jnp.maximum(m2[:groups, :], m3[:groups, :])
+    )
+    spots, row = {}, 0
+    for out in (e_ref, a_ref, b_ref):
+        for at in range(0, out.shape[0], HALF):
+            spots[row + at] = (out, at)
+        row += out.shape[0]
+    for g in range(groups):
+        spread = scaled(scale_ref, g)
         for h in (0, 1):
             row = g * LANES + h * HALF
-            out, at = (a_ref, row) if row < rows else (b_ref, row - rows)
+            out, at = spots[row]
             factor = spread[h * HALF : (h + 1) * HALF, :]
             for k in range(fresh_ref.shape[1] // LANES):
                 lanes = slice(k * LANES, (k + 1) * LANES)
                 out[at : at + HALF, lanes] = (fresh_ref[row : row + HALF, lanes] * factor).astype(BF16)
+
+
+def early_kernel(r_ref, l_ref, scale_ref, r_out, l_out):
+    for g in range(r_ref.shape[0] // LANES):
+        spread = scaled(scale_ref, g)
+        rows = slice(g * LANES, (g + 1) * LANES)
+        for ref, out in ((r_ref, r_out), (l_ref, l_out)):
+            for k in range(ref.shape[1] // LANES):
+                lanes = slice(k * LANES, (k + 1) * LANES)
+                out[rows, lanes] = (ref[rows, lanes] * spread).astype(BF16)
 
 
 def spot(piece, out, back, row, sem):
@@ -111,15 +132,16 @@
     return pltpu.make_async_copy(piece, out.at[0, pl.ds(row, piece.shape[0]), cols], sem)
 
 
-def own_kernel(groups, a_ref, b_ref, fresh_ref, scale_ref, out, fresh_out, scale_out, line, sems):
+def own_kernel(groups, e_ref, a_ref, b_ref, fresh_ref, scale_ref, out, fresh_out, scale_out, line, sems):
     for g in range(groups):
         line[:, g * LANES : (g + 1) * LANES] = scale_ref[g : g + 1, :]
-    run([
-        spot(a_ref, out, 0, 0, sems.at[0]),
-        spot(b_ref, out, 0, a_ref.shape[0], sems.at[1]),
-        pltpu.make_async_copy(fresh_ref, fresh_out.at[0], sems.at[2]),
-        pltpu.make_async_copy(line, scale_out, sems.at[3]),
-    ])
+    copies, row = [], 0
+    for piece in (e_ref, a_ref, b_ref):
+        copies.append(spot(piece, out, 0, row, sems.at[len(copies)]))
+        row += piece.shape[0]
+    copies.append(pltpu.make_async_copy(fresh_ref, fresh_out.at[0], sems.at[3]))
+    copies.append(pltpu.make_async_copy(line, scale_out, sems.at[4]))
+    run(copies)
 
 
 def place_kernel(spots, *refs):
@@ -145,9 +167,10 @@
     for yk in RING:
         for ck in range(CORES):
             row = CORES * (y ^ yk) + (c ^ ck)
-            for xk in RING:
+            for back in range(xs):
+                col = lax.rem(x + (xs - back), xs)
                 for k in range(part):
-                    buf[pl.ds((row * xs + (x ^ xk)) * part + k, 1), :] = lines[at : at + 1, :]
+                    buf[pl.ds((row * xs + col) * part + k, 1), :] = lines[at : at + 1, :]
                     at += 1
     for j in range(xs * part):
         out[:, j * LANES : (j + 1) * LANES] = buf[pl.ds(j, CORES * YS, stride=xs * part), :].astype(BF16)
@@ -168,7 +191,10 @@
 
 def body(w_down, avg_down, router_weight, router_gain):
     _, rows, cols = w_down.shape
-    groups, half = rows // LANES, rows // 2
+    groups = rows // LANES
+    ne = LANES
+    na = (rows - 2 * ne) // 2
+    nb = rows - ne - na
     xs, eps = lax.axis_size("fsdp"), lax.axis_size("ep")
     per, part = CORES * YS, cols // LANES
 
@@ -181,40 +207,46 @@
     def swap(v, step):
         return stacked(v, move(v, "ep", lambda e: e ^ step))
 
-    fresh, msg = call(
+    fresh, early, msg = call(
         functools.partial(fresh_kernel, groups),
         (in_hbm(w_down), in_hbm(avg_down), in_hbm(router_weight.reshape(1, -1)), in_hbm(router_gain.reshape(1, -1))),
         [ANY] * 4,
-        (pltpu.VMEM((rows, cols), F32), pltpu.VMEM((groups + part, LANES), F32)),
-        (VM, VM),
+        (pltpu.VMEM((rows, cols), F32), pltpu.VMEM((ne, cols), F32), pltpu.VMEM((groups + part, LANES), F32)),
+        (VM,) * 3,
         [
             pltpu.VMEM((rows, cols), F32), pltpu.VMEM((rows, cols), F32), pltpu.VMEM((2, cols), F32),
             pltpu.SemaphoreType.DMA((2, groups)), pltpu.SemaphoreType.DMA((2,)),
         ],
     )
-    other = move(msg, "fsdp", lambda i: i ^ 1)
-    msg = jnp.concatenate([jnp.maximum(msg[:groups], other[:groups]), msg[groups:], other[groups:]], 0)
-    other = move(msg, "fsdp", lambda i: i ^ 3)
-    a, b, scale = call(
+    m2, m1, m3 = shift(msg, 2), shift(msg, 1), shift(msg, -1)
+    e_r, e_l = shift(early, 1), shift(early, -1)
+    e, a, b, scale = call(
         functools.partial(serve_kernel, groups),
-        (in_vmem(fresh), in_vmem(msg), in_vmem(other)), [VM] * 3,
-        (pltpu.VMEM((half, cols), BF16), pltpu.VMEM((half, cols), BF16), pltpu.VMEM((groups, LANES), F32)), (VM,) * 3,
+        [in_vmem(v) for v in (fresh, msg, m1, m2, m3)], [VM] * 5,
+        (*(pltpu.VMEM((n, cols), BF16) for n in (ne, na, nb)), pltpu.VMEM((groups, LANES), F32)), (VM,) * 4,
     )
     a_r, b_l = shift(a, 1), shift(b, -1)
     b_r, a_l = shift(b, 1), shift(a, -1)
+    e_r, e_l = call(
+        early_kernel,
+        [in_vmem(v) for v in (e_r, e_l, scale)], [VM] * 3,
+        (pltpu.VMEM((ne, cols), BF16),) * 2, (VM,) * 2,
+    )
+    e_rr = shift(e_r, 1)
     a_rr, b_ll = shift(a_r, 1), shift(b_l, -1)
 
     out, fresh_out, scale_out = call(
         functools.partial(own_kernel, groups),
-        [in_vmem(v) for v in (a, b, fresh, scale)], [VM] * 4,
+        [in_vmem(v) for v in (e, a, b, fresh, scale)], [VM] * 5,
         (pltpu.HBM((1, rows, cols * xs), BF16), pltpu.HBM((1, rows, cols), F32), pltpu.HBM((1, rows), F32)), (ANY,) * 3,
-        [pltpu.VMEM((1, rows), F32), pltpu.SemaphoreType.DMA((4,))],
-    )
-    out = place(out, [a_r, b_l], [(1, 0), (3, half)])
-    out = place(out, [b_r, a_l], [(1, half), (3, 0)])
-    out = place(out, [a_rr, b_ll], [(2, 0), (2, half)])
-
-    lines = stacked(msg[groups:], other[groups:])
+        [pltpu.VMEM((1, rows), F32), pltpu.SemaphoreType.DMA((5,))],
+    )
+    at_a, at_b = ne, ne + na
+    out = place(out, [e_r, e_l, a_r, b_l], [(1, 0), (3, 0), (1, at_a), (3, at_b)])
+    out = place(out, [b_r, a_l, e_rr], [(1, at_b), (3, at_a), (2, 0)])
+    out = place(out, [a_rr, b_ll], [(2, at_a), (2, at_b)])
+
+    lines = stacked(stacked(msg[groups:], m1[groups:]), stacked(m2[groups:], m3[groups:]))
     lines = swap(lines, 1)
     lines = swap(lines, CORES)
     lines = swap(lines, CORES * 3)

time: 61.8 us -> 87.1 us (1.41)
  the two profiles are of different devices: /device:TPU:134 before, /device:TPU:1 now
where the time goes in v3:
time: 87.1 us; the launch traced here: 86.7 us
  waiting for transfers between devices  45.7 us (52%)
  starting transfers between devices  30.4 us (35%)
  Pallas kernels  9.72 us (11%)
    ppermute x18, waiting for transfers between devices, move(): lax.ppermute(v, axis, [(i, to(i)) for i in range(lax.axis_size(axis))])  45.7 us
    ppermute x18, starting transfers between devices, move(): lax.ppermute(v, axis, [(i, to(i)) for i in range(lax.axis_size(axis))])  30.4 us
    pallas_call x9, Pallas kernels, call(): pl.pallas_call(kernel, out_shape=outs, in_specs=in_specs, out_specs=out_s...  9.72 us
  transfers between devices with their start and end apart: 18, of which 9 were waited for; matrix products, arithmetic and copies ran while one was open for 0% of the time, Pallas kernels for 6%

profile of v3, /device:TPU:1, one launch (start us, length us, event | category | flops | bytes accessed | tf_op | source)
XLA Modules:
  0.0 86.7 jit_solution(12909560727136792751)
XLA Ops:
  0.6 3.0 %shard_map.75 = (f32[1408,512]{1,0:T(8,128)S(1)}, f32[128,512]{1,0:T(8,128)S(1)}, f32[15,128]{1,0:T(8,128)S(1)}) custom-call(f32[1,1408,512]{2,1,0:T(8,128)} %w_hbm.1, f32[1,1408,512]{2,1,0:T(8,128)} %a_hbm.1, f32[1,512]{1,0:T(1,128)} %bitcast.4, f32[1,512]{1,0:T(1,128)} %bitcast.5), custom_call_target="tpu_custom_call" | custom-call | tf_op jit(solution)/shard_map/pallas_call | solution.py:30
  3.6 2.1 %collective-permute-start = (f32[15,128]{1,0:T(8,128)S(1)}, f32[15,128]{1,0:T(8,128)S(1)}, u32[]{:S(2)}, u32[]{:S(2)}) collective-permute-start(f32[15,128]{1,0:T(8,128)S(1)} %get-tuple-element.17.m0), channel_id=1, source_target_pairs={{0,1},{1,2},{2,3},{3,0},{4,5},{5,6},{6,7},{7,4},{8,9},{9,10},{10,1... | collective-permute-start | bytes 23048 | tf_op jit(solution)/shard_map/ppermute | solution.py:202
  5.7 2.5 %collective-permute-start.1 = (f32[15,128]{1,0:T(8,128)S(1)}, f32[15,128]{1,0:T(8,128)S(1)}, u32[]{:S(2)}, u32[]{:S(2)}) collective-permute-start(f32[15,128]{1,0:T(8,128)S(1)} %get-tuple-element.17.m0), channel_id=1, source_target_pairs={{0,2},{1,3},{2,0},{3,1},{4,6},{5,7},{6,4},{7,5},{8,10},{9,11},{10,... | collective-permute-start | bytes 23048 | tf_op jit(solution)/shard_map/ppermute | solution.py:202
  8.1 1.2 %collective-permute-start.2 = (f32[15,128]{1,0:T(8,128)S(1)}, f32[15,128]{1,0:T(8,128)S(1)}, u32[]{:S(2)}, u32[]{:S(2)}) collective-permute-start(f32[15,128]{1,0:T(8,128)S(1)} %get-tuple-element.17.m0), channel_id=1, source_target_pairs={{0,3},{1,0},{2,1},{3,2},{4,7},{5,4},{6,5},{7,6},{8,11},{9,8},{10,9... | collective-permute-start | bytes 23048 | tf_op jit(solution)/shard_map/ppermute | solution.py:202
  9.3 0.4 collective-permute-done.1.m2
  9.7 1.2 %collective-permute-done.2.m3 = f32[15,128]{1,0:T(8,128)S(1)} collective-permute-done((f32[15,128]{1,0:T(8,128)S(1)}, f32[15,128]{1,0:T(8,128)S(1)}, u32[]{:S(2)}, u32[]{:S(2)}) %collective-permute-start.2) | collective-permute-done | bytes 7712 | tf_op jit(solution)/shard_map/ppermute | solution.py:202
  10.9 0.3 shard_map.76
  11.3 2.1 %collective-permute-start.5 = (bf16[704,512]{1,0:T(8,128)(2,1)S(1)}, bf16[704,512]{1,0:T(8,128)(2,1)S(1)}, u32[]{:S(2)}, u32[]{:S(2)}) collective-permute-start(bf16[704,512]{1,0:T(8,128)(2,1)S(1)} %get-tuple-element.19.b_ref), channel_id=1, source_target_pairs={{0,3},{1,0},{2,1},{3,2},{4,7},{5,4},{6,5},{7,6},{8,11},{9,8},{10,9... | collective-permute-start | bytes 2162696 | tf_op jit(solution)/shard_map/ppermute | solution.py:202
  13.5 2.8 %collective-permute-start.12 = (f32[16,128]{1,0:T(8,128)S(1)}, f32[16,128]{1,0:T(8,128)S(1)}, u32[]{:S(2)}, u32[]{:S(2)}) collective-permute-start(f32[16,128]{1,0:T(8,128)S(1)} %fusion), channel_id=1, source_target_pairs={{0,4},{4,0},{8,12},{12,8},{16,20},{20,16},{24,28},{28,24},{32,36},... | collective-permute-start | bytes 24584 | tf_op jit(solution)/shard_map/ppermute | solution.py:202
  16.2 0.8 collective-permute-done.12
  17.0 1.3 %collective-permute-start.13 = (f32[32,128]{1,0:T(8,128)S(1)}, f32[32,128]{1,0:T(8,128)S(1)}, u32[]{:S(2)}, u32[]{:S(2)}) collective-permute-start(f32[32,128]{1,0:T(8,128)S(1)} %pad_maximum_fusion.4), channel_id=1, source_target_pairs={{0,8},{4,12},{8,0},{12,4},{16,24},{20,28},{24,16},{28,20},{32,40},... | collective-permute-start | bytes 49160 | tf_op jit(solution)/shard_map/ppermute | solution.py:202
  18.3 1.6 %collective-permute-done.13 = f32[32,128]{1,0:T(8,128)S(1)} collective-permute-done((f32[32,128]{1,0:T(8,128)S(1)}, f32[32,128]{1,0:T(8,128)S(1)}, u32[]{:S(2)}, u32[]{:S(2)}) %collective-permute-start.13) | collective-permute-done | bytes 16416 | tf_op jit(solution)/shard_map/ppermute | solution.py:202
  19.9 2.7 %collective-permute-start.14 = (f32[64,128]{1,0:T(8,128)S(1)}, f32[64,128]{1,0:T(8,128)S(1)}, u32[]{:S(2)}, u32[]{:S(2)}) collective-permute-start(f32[64,128]{1,0:T(8,128)S(1)} %pad_maximum_fusion.3), channel_id=1, source_target_pairs={{0,24},{4,28},{8,16},{12,20},{16,8},{20,12},{24,0},{28,4},{32,56},... | collective-permute-start | bytes 98312 | tf_op jit(solution)/shard_map/ppermute | solution.py:202
  22.7 1.6 %collective-permute-done.14 = f32[64,128]{1,0:T(8,128)S(1)} collective-permute-done((f32[64,128]{1,0:T(8,128)S(1)}, f32[64,128]{1,0:T(8,128)S(1)}, u32[]{:S(2)}, u32[]{:S(2)}) %collective-permute-start.14) | collective-permute-done | bytes 32800 | tf_op jit(solution)/shard_map/ppermute | solution.py:202
  24.3 1.7 %collective-permute-start.15 = (bf16[8,2048]{1,0:T(8,128)(2,1)S(1)}, bf16[8,2048]{1,0:T(8,128)(2,1)S(1)}, u32[]{:S(2)}, u32[]{:S(2)}) collective-permute-start(bf16[8,2048]{1,0:T(8,128)(2,1)S(1)} %shard_map.82), channel_id=1, source_target_pairs={{0,32},{4,36},{8,40},{12,44},{16,48},{20,52},{24,56},{28,60},{32,0... | collective-permute-start | bytes 98312 | tf_op jit(solution)/shard_map/ppermute | solution.py:202
  26.1 1.0 %collective-permute-start.10 = (f32[128,512]{1,0:T(8,128)S(1)}, f32[128,512]{1,0:T(8,128)S(1)}, u32[]{:S(2)}, u32[]{:S(2)}) collective-permute-start(f32[128,512]{1,0:T(8,128)S(1)} %get-tuple-element.20), channel_id=1, source_target_pairs={{0,3},{1,0},{2,1},{3,2},{4,7},{5,4},{6,5},{7,6},{8,11},{9,8},{10,9... | collective-permute-start | bytes 786440 | tf_op jit(solution)/shard_map/ppermute | solution.py:202
  27.1 0.4 collective-permute-start.7
  27.5 2.4 %collective-permute-start.6 = (bf16[704,512]{1,0:T(8,128)(2,1)S(1)}, bf16[704,512]{1,0:T(8,128)(2,1)S(1)}, u32[]{:S(2)}, u32[]{:S(2)}) collective-permute-start(bf16[704,512]{1,0:T(8,128)(2,1)S(1)} %collective-permute-done.5.refs_3_), channel_id=1, source_target_pairs={{0,3},{1,0},{2,1},{3,2},{4,7},{5,4},{6,5},{7,6},{8,11},{9,8},{10,9... | collective-permute-start | bytes 2162696 | tf_op jit(solution)/shard_map/ppermute | solution.py:202
  29.9 3.1 %collective-permute-start.16 = (bf16[16,2048]{1,0:T(8,128)(2,1)S(1)}, bf16[16,2048]{1,0:T(8,128)(2,1)S(1)}, u32[]{:S(2)}, u32[]{:S(2)}) collective-permute-start(bf16[16,2048]{1,0:T(8,128)(2,1)S(1)} %pad_maximum_fusion.1), channel_id=1, source_target_pairs={{0,64},{4,68},{8,72},{12,76},{16,80},{20,84},{24,88},{28,92},{32,9... | collective-permute-start | bytes 196616 | tf_op jit(solution)/shard_map/ppermute | solution.py:202
  33.0 2.0 %collective-permute-done.16 = bf16[16,2048]{1,0:T(8,128)(2,1)S(1)} collective-permute-done((bf16[16,2048]{1,0:T(8,128)(2,1)S(1)}, bf16[16,2048]{1,0:T(8,128)(2,1)S(1)}, u32[]{:S(2)}, u32[]{:S(2)}) %collective-permute-start.16) | collective-permute-done | bytes 65568 | tf_op jit(solution)/shard_map/ppermute | solution.py:202
  35.0 1.5 %collective-permute-start.4 = (bf16[576,512]{1,0:T(8,128)(2,1)S(1)}, bf16[576,512]{1,0:T(8,128)(2,1)S(1)}, u32[]{:S(2)}, u32[]{:S(2)}) collective-permute-start(bf16[576,512]{1,0:T(8,128)(2,1)S(1)} %collective-permute-done.3.refs_2_), channel_id=1, source_target_pairs={{0,1},{1,2},{2,3},{3,0},{4,5},{5,6},{6,7},{7,4},{8,9},{9,10},{10,1... | collective-permute-start | bytes 1769480 | tf_op jit(solution)/shard_map/ppermute | solution.py:202
  36.5 0.1 collective-permute-start.9
  36.5 31.0 %collective-permute-done.9.r_ref = f32[128,512]{1,0:T(8,128)S(1)} collective-permute-done((f32[128,512]{1,0:T(8,128)S(1)}, f32[128,512]{1,0:T(8,128)S(1)}, u32[]{:S(2)}, u32[]{:S(2)}) %collective-permute-start.9) | collective-permute-done | bytes 262176 | tf_op jit(solution)/shard_map/ppermute | solution.py:202
  67.5 5.6 %collective-permute-start.17 = (bf16[32,2048]{1,0:T(8,128)(2,1)S(1)}, bf16[32,2048]{1,0:T(8,128)(2,1)S(1)}, u32[]{:S(2)}, u32[]{:S(2)}) collective-permute-start(bf16[32,2048]{1,0:T(8,128)(2,1)S(1)} %pad_maximum_fusion.refs_0_), channel_id=1, source_target_pairs={{0,224},{4,228},{8,232},{12,236},{16,240},{20,244},{24,248},{28,25... | collective-permute-start | bytes 393224 | tf_op jit(solution)/shard_map/ppermute | solution.py:202
  73.1 0.1 shard_map.77
  73.2 6.2 %collective-permute-done.17.refs_1_ = bf16[32,2048]{1,0:T(8,128)(2,1)S(1)} collective-permute-done((bf16[32,2048]{1,0:T(8,128)(2,1)S(1)}, bf16[32,2048]{1,0:T(8,128)(2,1)S(1)}, u32[]{:S(2)}, u32[]{:S(2)}) %collective-permute-start.17) | collective-permute-done | bytes 131104 | tf_op jit(solution)/shard_map/ppermute | solution.py:202
  79.4 2.1 %shard_map.78 = (bf16[1,1408,2048]{2,1,0:T(8,128)(2,1)}, f32[1,1408,512]{2,1,0:T(8,128)}, f32[1,1408]{1,0:T(1,128)}) custom-call(bf16[128,512]{1,0:T(8,128)(2,1)S(1)} %get-tuple-element.24.e_ref, bf16[576,512]{1,0:T(8,128)(2,1)S(1)} %get-tuple-element.18.a_ref, bf16[704,512]{1,0:T(8,128)(2,1)S(1)} %get-tuple-element.19.b_ref, ...), custom_call_target="tpu_custom_call" | custom-call | tf_op jit(solution)/shard_map/pallas_call | solution.py:30
  81.5 0.8 shard_map.83
  82.3 1.2 %shard_map.79.refs_3_ = bf16[1,1408,2048]{2,1,0:T(8,128)(2,1)} custom-call(bf16[128,512]{1,0:T(8,128)(2,1)S(1)} %get-tuple-element.22.refs_0_, bf16[128,512]{1,0:T(8,128)(2,1)S(1)} %get-tuple-element.23.refs_1_, bf16[576,512]{1,0:T(8,128)(2,1)S(1)} %collective-permute-done.3.refs_2_, ...), custom_call_target="tpu_custom_call", output_to_operand_aliasing={{}: (4, {})} | custom-call | tf_op jit(solution)/shard_map/pallas_call | solution.py:30
  83.5 0.9 %collective-permute-done.11.refs_2_ = bf16[128,512]{1,0:T(8,128)(2,1)S(1)} collective-permute-done((bf16[128,512]{1,0:T(8,128)(2,1)S(1)}, bf16[128,512]{1,0:T(8,128)(2,1)S(1)}, u32[]{:S(2)}, u32[]{:S(2)}) %collective-permute-start.11) | collective-permute-done | bytes 131104 | tf_op jit(solution)/shard_map/ppermute | solution.py:202
  84.4 1.1 %shard_map.80.refs_2_ = bf16[1,1408,2048]{2,1,0:T(8,128)(2,1)} custom-call(bf16[704,512]{1,0:T(8,128)(2,1)S(1)} %collective-permute-done.7.refs_0_, bf16[576,512]{1,0:T(8,128)(2,1)S(1)} %collective-permute-done.8.refs_1_, bf16[128,512]{1,0:T(8,128)(2,1)S(1)} %collective-permute-done.11.refs_2_, ...), custom_call_target="tpu_custom_call", output_to_operand_aliasing={{}: (3, {})} | custom-call | tf_op jit(solution)/shard_map/pallas_call | solution.py:30
  85.6 1.1 %shard_map.81 = bf16[1,1408,2048]{2,1,0:T(8,128)(2,1)} custom-call(bf16[576,512]{1,0:T(8,128)(2,1)S(1)} %collective-permute-done.4.refs_0_, bf16[704,512]{1,0:T(8,128)(2,1)S(1)} %collective-permute-done.6.refs_1_, bf16[1,1408,2048]{2,1,0:T(8,128)(2,1)} %shard_map.80.refs_2_), custom_call_target="tpu_custom_call", output_to_operand_aliasing={{}: (2, {})} | custom-call | tf_op jit(solution)/shard_map/pallas_call | solution.py:30
  (23 shorter events, 0.2 us)
Async XLA Ops:
  3.6 5.7 %collective-permute-start = (f32[15,128]{1,0:T(8,128)S(1)}, f32[15,128]{1,0:T(8,128)S(1)}, u32[]{:S(2)}, u32[]{:S(2)}) collective-permute-start(f32[15,128]{1,0:T(8,128)S(1)} %get-tuple-element.17.m0), channel_id=1, source_target_pairs={{0,1},{1,2},{2,3},{3,0},{4,5},{5,6},{6,7},{7,4},{8,9},{9,10},{10,1... | collective-permute-start | bytes 23048 | tf_op jit(solution)/shard_map/ppermute | solution.py:202
  5.7 4.0 %collective-permute-start.1 = (f32[15,128]{1,0:T(8,128)S(1)}, f32[15,128]{1,0:T(8,128)S(1)}, u32[]{:S(2)}, u32[]{:S(2)}) collective-permute-start(f32[15,128]{1,0:T(8,128)S(1)} %get-tuple-element.17.m0), channel_id=1, source_target_pairs={{0,2},{1,3},{2,0},{3,1},{4,6},{5,7},{6,4},{7,5},{8,10},{9,11},{10,... | collective-permute-start | bytes 23048 | tf_op jit(solution)/shard_map/ppermute | solution.py:202
  8.1 2.8 %collective-permute-start.2 = (f32[15,128]{1,0:T(8,128)S(1)}, f32[15,128]{1,0:T(8,128)S(1)}, u32[]{:S(2)}, u32[]{:S(2)}) collective-permute-start(f32[15,128]{1,0:T(8,128)S(1)} %get-tuple-element.17.m0), channel_id=1, source_target_pairs={{0,3},{1,0},{2,1},{3,2},{4,7},{5,4},{6,5},{7,6},{8,11},{9,8},{10,9... | collective-permute-start | bytes 23048 | tf_op jit(solution)/shard_map/ppermute | solution.py:202
  11.3 16.3 %collective-permute-start.5 = (bf16[704,512]{1,0:T(8,128)(2,1)S(1)}, bf16[704,512]{1,0:T(8,128)(2,1)S(1)}, u32[]{:S(2)}, u32[]{:S(2)}) collective-permute-start(bf16[704,512]{1,0:T(8,128)(2,1)S(1)} %get-tuple-element.19.b_ref), channel_id=1, source_target_pairs={{0,3},{1,0},{2,1},{3,2},{4,7},{5,4},{6,5},{7,6},{8,11},{9,8},{10,9... | collective-permute-start | bytes 2162696 | tf_op jit(solution)/shard_map/ppermute | solution.py:202
  13.5 3.6 %collective-permute-start.12 = (f32[16,128]{1,0:T(8,128)S(1)}, f32[16,128]{1,0:T(8,128)S(1)}, u32[]{:S(2)}, u32[]{:S(2)}) collective-permute-start(f32[16,128]{1,0:T(8,128)S(1)} %fusion), channel_id=1, source_target_pairs={{0,4},{4,0},{8,12},{12,8},{16,20},{20,16},{24,28},{28,24},{32,36},... | collective-permute-start | bytes 24584 | tf_op jit(solution)/shard_map/ppermute | solution.py:202
  17.0 2.9 %collective-permute-start.13 = (f32[32,128]{1,0:T(8,128)S(1)}, f32[32,128]{1,0:T(8,128)S(1)}, u32[]{:S(2)}, u32[]{:S(2)}) collective-permute-start(f32[32,128]{1,0:T(8,128)S(1)} %pad_maximum_fusion.4), channel_id=1, source_target_pairs={{0,8},{4,12},{8,0},{12,4},{16,24},{20,28},{24,16},{28,20},{32,40},... | collective-permute-start | bytes 49160 | tf_op jit(solution)/shard_map/ppermute | solution.py:202
  18.3 16.6 %collective-permute-start.3 = (bf16[576,512]{1,0:T(8,128)(2,1)S(1)}, bf16[576,512]{1,0:T(8,128)(2,1)S(1)}, u32[]{:S(2)}, u32[]{:S(2)}) collective-permute-start(bf16[576,512]{1,0:T(8,128)(2,1)S(1)} %get-tuple-element.18.a_ref), channel_id=1, source_target_pairs={{0,1},{1,2},{2,3},{3,0},{4,5},{5,6},{6,7},{7,4},{8,9},{9,10},{10,1... | collective-permute-start | bytes 1769480 | tf_op jit(solution)/shard_map/ppermute | solution.py:202
  19.9 4.3 %collective-permute-start.14 = (f32[64,128]{1,0:T(8,128)S(1)}, f32[64,128]{1,0:T(8,128)S(1)}, u32[]{:S(2)}, u32[]{:S(2)}) collective-permute-start(f32[64,128]{1,0:T(8,128)S(1)} %pad_maximum_fusion.3), channel_id=1, source_target_pairs={{0,24},{4,28},{8,16},{12,20},{16,8},{20,12},{24,0},{28,4},{32,56},... | collective-permute-start | bytes 98312 | tf_op jit(solution)/shard_map/ppermute | solution.py:202
  24.3 5.6 %collective-permute-start.15 = (bf16[8,2048]{1,0:T(8,128)(2,1)S(1)}, bf16[8,2048]{1,0:T(8,128)(2,1)S(1)}, u32[]{:S(2)}, u32[]{:S(2)}) collective-permute-start(bf16[8,2048]{1,0:T(8,128)(2,1)S(1)} %shard_map.82), channel_id=1, source_target_pairs={{0,32},{4,36},{8,40},{12,44},{16,48},{20,52},{24,56},{28,60},{32,0... | collective-permute-start | bytes 98312 | tf_op jit(solution)/shard_map/ppermute | solution.py:202
  26.1 10.4 %collective-permute-start.10 = (f32[128,512]{1,0:T(8,128)S(1)}, f32[128,512]{1,0:T(8,128)S(1)}, u32[]{:S(2)}, u32[]{:S(2)}) collective-permute-start(f32[128,512]{1,0:T(8,128)S(1)} %get-tuple-element.20), channel_id=1, source_target_pairs={{0,3},{1,0},{2,1},{3,2},{4,7},{5,4},{6,5},{7,6},{8,11},{9,8},{10,9... | collective-permute-start | bytes 786440 | tf_op jit(solution)/shard_map/ppermute | solution.py:202
  27.1 57.3 %collective-permute-start.7 = (bf16[704,512]{1,0:T(8,128)(2,1)S(1)}, bf16[704,512]{1,0:T(8,128)(2,1)S(1)}, u32[]{:S(2)}, u32[]{:S(2)}) collective-permute-start(bf16[704,512]{1,0:T(8,128)(2,1)S(1)} %get-tuple-element.19.b_ref), channel_id=1, source_target_pairs={{0,1},{1,2},{2,3},{3,0},{4,5},{5,6},{6,7},{7,4},{8,9},{9,10},{10,1... | collective-permute-start | bytes 2162696 | tf_op jit(solution)/shard_map/ppermute | solution.py:202
  27.5 58.0 %collective-permute-start.6 = (bf16[704,512]{1,0:T(8,128)(2,1)S(1)}, bf16[704,512]{1,0:T(8,128)(2,1)S(1)}, u32[]{:S(2)}, u32[]{:S(2)}) collective-permute-start(bf16[704,512]{1,0:T(8,128)(2,1)S(1)} %collective-permute-done.5.refs_3_), channel_id=1, source_target_pairs={{0,3},{1,0},{2,1},{3,2},{4,7},{5,4},{6,5},{7,6},{8,11},{9,8},{10,9... | collective-permute-start | bytes 2162696 | tf_op jit(solution)/shard_map/ppermute | solution.py:202
  29.9 5.0 %collective-permute-start.16 = (bf16[16,2048]{1,0:T(8,128)(2,1)S(1)}, bf16[16,2048]{1,0:T(8,128)(2,1)S(1)}, u32[]{:S(2)}, u32[]{:S(2)}) collective-permute-start(bf16[16,2048]{1,0:T(8,128)(2,1)S(1)} %pad_maximum_fusion.1), channel_id=1, source_target_pairs={{0,64},{4,68},{8,72},{12,76},{16,80},{20,84},{24,88},{28,92},{32,9... | collective-permute-start | bytes 196616 | tf_op jit(solution)/shard_map/ppermute | solution.py:202
  35.0 49.5 %collective-permute-start.8 = (bf16[576,512]{1,0:T(8,128)(2,1)S(1)}, bf16[576,512]{1,0:T(8,128)(2,1)S(1)}, u32[]{:S(2)}, u32[]{:S(2)}) collective-permute-start(bf16[576,512]{1,0:T(8,128)(2,1)S(1)} %get-tuple-element.18.a_ref), channel_id=1, source_target_pairs={{0,3},{1,0},{2,1},{3,2},{4,7},{5,4},{6,5},{7,6},{8,11},{9,8},{10,9... | collective-permute-start | bytes 1769480 | tf_op jit(solution)/shard_map/ppermute | solution.py:202
  35.0 50.6 %collective-permute-start.4 = (bf16[576,512]{1,0:T(8,128)(2,1)S(1)}, bf16[576,512]{1,0:T(8,128)(2,1)S(1)}, u32[]{:S(2)}, u32[]{:S(2)}) collective-permute-start(bf16[576,512]{1,0:T(8,128)(2,1)S(1)} %collective-permute-done.3.refs_2_), channel_id=1, source_target_pairs={{0,1},{1,2},{2,3},{3,0},{4,5},{5,6},{6,7},{7,4},{8,9},{9,10},{10,1... | collective-permute-start | bytes 1769480 | tf_op jit(solution)/shard_map/ppermute | solution.py:202
  36.5 31.1 %collective-permute-start.9 = (f32[128,512]{1,0:T(8,128)S(1)}, f32[128,512]{1,0:T(8,128)S(1)}, u32[]{:S(2)}, u32[]{:S(2)}) collective-permute-start(f32[128,512]{1,0:T(8,128)S(1)} %get-tuple-element.20), channel_id=1, source_target_pairs={{0,1},{1,2},{2,3},{3,0},{4,5},{5,6},{6,7},{7,4},{8,9},{9,10},{10,1... | collective-permute-start | bytes 786440 | tf_op jit(solution)/shard_map/ppermute | solution.py:202
  67.5 11.9 %collective-permute-start.17 = (bf16[32,2048]{1,0:T(8,128)(2,1)S(1)}, bf16[32,2048]{1,0:T(8,128)(2,1)S(1)}, u32[]{:S(2)}, u32[]{:S(2)}) collective-permute-start(bf16[32,2048]{1,0:T(8,128)(2,1)S(1)} %pad_maximum_fusion.refs_0_), channel_id=1, source_target_pairs={{0,224},{4,228},{8,232},{12,236},{16,240},{20,244},{24,248},{28,25... | collective-permute-start | bytes 393224 | tf_op jit(solution)/shard_map/ppermute | solution.py:202
  79.4 5.0 %collective-permute-start.11 = (bf16[128,512]{1,0:T(8,128)(2,1)S(1)}, bf16[128,512]{1,0:T(8,128)(2,1)S(1)}, u32[]{:S(2)}, u32[]{:S(2)}) collective-permute-start(bf16[128,512]{1,0:T(8,128)(2,1)S(1)} %get-tuple-element.22.refs_0_), channel_id=1, source_target_pairs={{0,1},{1,2},{2,3},{3,0},{4,5},{5,6},{6,7},{7,4},{8,9},{9,10},{10,1... | collective-permute-start | bytes 393224 | tf_op jit(solution)/shard_map/ppermute | solution.py:202

commit v4 on v2

v4 whole, which is shorter than its diff:
```python
import functools

import jax
import jax.numpy as jnp
from jax import lax
from jax.experimental import pallas as pl
from jax.experimental.pallas import tpu as pltpu
from jax.sharding import PartitionSpec as P


F32, BF16 = jnp.float32, jnp.bfloat16
ANY = pl.BlockSpec(memory_space=pl.ANY)
VM = pl.BlockSpec(memory_space=pltpu.VMEM)
LANES = 128
HALF = LANES // 2
CORES, YS, ZS = 2, 4, 8
RING = (0, 1, 3, 2)
TOWER = (0, 1, 2, 3, 7, 6, 5, 4)
STEPS, MIDDLE = 248.0, 124.0
TINY = 1e-30


def in_vmem(x):
    return pltpu.with_memory_space_constraint(x, pltpu.VMEM)


def in_hbm(x):
    return pltpu.with_memory_space_constraint(x, pltpu.HBM)


def call(kernel, ins, in_specs, outs, out_specs, scratch=(), aliases=None):
    return pl.pallas_call(
        kernel,
        out_shape=outs,
        in_specs=in_specs,
        out_specs=out_specs,
        scratch_shapes=list(scratch),
        input_output_aliases=aliases or {},
        compiler_params=pltpu.CompilerParams(vmem_limit_bytes=12 * 1024 * 1024),
    )(*ins)


def stacked(one, two):
    low = jnp.array(-jnp.inf, one.dtype)
    return jnp.maximum(
        lax.pad(one, low, ((0, two.shape[0], 0), (0, 0, 0))),
        lax.pad(two, low, ((one.shape[0], 0, 0), (0, 0, 0))),
    )


def run(copies):
    for copy in copies:
        copy.start()
    for copy in copies:
        copy.wait()


def spread(line):
    return jnp.broadcast_to(line, (LANES, LANES)).T


def lanes_of(width):
    return [slice(k * LANES, (k + 1) * LANES) for k in range(width // LANES)]


def fresh_kernel(start, groups, chunks, router, w_hbm, a_hbm, *refs):
    refs = list(refs)
    r_hbm = [refs.pop(0) for _ in range(2 * router)]
    fresh_ref, top_ref = refs.pop(0), refs.pop(0)
    outs = [refs.pop(0) for _ in chunks]
    w_buf, a_buf, r_buf, sems, r_sems = refs

    def copies(g):
        there, here = pl.ds(start + g * LANES, LANES), pl.ds(g * LANES, LANES)
        return (
            pltpu.make_async_copy(w_hbm.at[0, there, :], w_buf.at[here, :], sems.at[0, g]),
            pltpu.make_async_copy(a_hbm.at[0, there, :], a_buf.at[here, :], sems.at[1, g]),
        )

    part = [pltpu.make_async_copy(ref, r_buf.at[k : k + 1, :], r_sems.at[k]) for k, ref in enumerate(r_hbm)]
    for g in range(groups):
        for copy in copies(g):
            copy.start()
    for copy in part:
        copy.start()
    blocks = lanes_of(fresh_ref.shape[1])
    for g in range(groups):
        for copy in copies(g):
            copy.wait()
        rows = slice(g * LANES, (g + 1) * LANES)
        top = None
        for lanes in blocks:
            fresh = 0.5 * a_buf[rows, lanes] + 0.5 * w_buf[rows, lanes]
            fresh_ref[rows, lanes] = fresh
            size = jnp.abs(fresh)
            top = size if top is None else jnp.maximum(top, size)
        line = jnp.max(top.T, axis=0, keepdims=True)
        top_ref[g : g + 1, :] = line
        inverse = spread(STEPS / jnp.maximum(line, TINY))
        for h in (0, 1):
            row = g * LANES + h * HALF
            factor = inverse[h * HALF : (h + 1) * HALF, :]
            for lanes in blocks:
                x = fresh_ref[row : row + HALF, lanes]
                code = jnp.exp2(jnp.abs(x) * factor - MIDDLE)
                code = jnp.where(x < 0, -code, code).astype(BF16)
                for out, (first, end) in zip(outs, chunks):
                    if first <= row < end:
                        out[row - first : row - first + HALF, lanes] = code
    if router:
        for copy in part:
            copy.wait()
        product = r_buf[0:1, :] * r_buf[1:2, :]
        for k, lanes in enumerate(blocks):
            top_ref[groups + k : groups + k + 1, :] = product[:, lanes]


def largest(msgs, g):
    out = msgs[0][g : g + 1, :]
    for msg in msgs[1:]:
        out = jnp.maximum(out, msg[g : g + 1, :])
    return out


def spot(piece, out, back, row, sem):
    xs = lax.axis_size("fsdp")
    owner = lax.rem(lax.axis_index("fsdp") + (xs - back), xs)
    width = piece.shape[1]
    cols = pl.ds(pl.multiple_of(owner * width, width), width)
    return pltpu.make_async_copy(piece, out.at[0, pl.ds(row, piece.shape[0]), cols], sem)


def own_kernel(groups, first, m0, m1, m2, m3, f_ref, g_ref, out, fresh_out, scale_out, line, buf, sems):
    upper, lower = pl.ds(0, first), pl.ds(first, g_ref.shape[0])
    copies = [
        pltpu.make_async_copy(f_ref, fresh_out.at[0, upper, :], sems.at[0]),
        pltpu.make_async_copy(g_ref, fresh_out.at[0, lower, :], sems.at[1]),
    ]
    for copy in copies:
        copy.start()
    for g in range(groups):
        scale = largest((m0, m1, m2, m3), g)
        line[:, g * LANES : (g + 1) * LANES] = scale
        inverse = spread(1.0 / scale)
        ref, at = (f_ref, g * LANES) if g * LANES < first else (g_ref, g * LANES - first)
        for lanes in lanes_of(buf.shape[1]):
            buf[g * LANES : (g + 1) * LANES, lanes] = (ref[at : at + LANES, lanes] * inverse).astype(BF16)
    late = [spot(buf, out, 0, 0, sems.at[2]), pltpu.make_async_copy(line, scale_out, sems.at[3])]
    for copy in late:
        copy.start()
    for copy in copies + late:
        copy.wait()


def land_kernel(spots, m0, m1, m2, m3, *refs):
    n = len(spots)
    msgs = (m0, m1, m2, m3)
    pieces, out, bufs, sems = refs[:n], refs[-n - 2], refs[-n - 1 : -1], refs[-1]
    copies = []
    for i, (piece, buf, (back, row)) in enumerate(zip(pieces, bufs, spots)):
        factors = {}
        for at in range(0, piece.shape[0], HALF):
            g, h = divmod(row + at, LANES)
            if g not in factors:
                own = jnp.maximum(msgs[back][g : g + 1, :], TINY)
                factors[g] = spread(own / (STEPS * largest(msgs, g)))
            factor = factors[g][h : h + HALF, :]
            for lanes in lanes_of(piece.shape[1]):
                code = piece[at : at + HALF, lanes].astype(F32)
                size = (jnp.log2(jnp.abs(code)) + MIDDLE) * factor
                buf[at : at + HALF, lanes] = jnp.where(code < 0, -size, size).astype(BF16)
        copies.append(spot(buf, out, back, row, sems.at[i]))
        copies[-1].start()
    for copy in copies:
        copy.wait()


def land(out, msgs, pieces, spots):
    ins = [in_vmem(p) for p in (*msgs, *pieces)] + [out]
    n = len(pieces)
    return call(
        functools.partial(land_kernel, tuple(spots)),
        ins, [VM] * (4 + n) + [ANY], pltpu.HBM(out.shape, out.dtype), ANY,
        [*(pltpu.VMEM(p.shape, BF16) for p in pieces), pltpu.SemaphoreType.DMA((n,))], {4 + n: 0},
    )


def router_rows_kernel(part, lines, out, buf):
    x, e = lax.axis_index("fsdp"), lax.axis_index("ep")
    y, c = lax.rem(e // CORES, YS), lax.rem(e, CORES)
    xs = lax.axis_size("fsdp")
    at = 0
    for yk in RING:
        for ck in range(CORES):
            row = CORES * (y ^ yk) + (c ^ ck)
            for back in range(xs):
                col = lax.rem(x + (xs - back), xs)
                for k in range(part):
                    buf[pl.ds((row * xs + col) * part + k, 1), :] = lines[at : at + 1, :]
                    at += 1
    for j in range(xs * part):
        out[:, j * LANES : (j + 1) * LANES] = buf[pl.ds(j, CORES * YS, stride=xs * part), :].astype(BF16)


def router_place_kernel(*refs):
    pieces, out, sems = refs[:-2], refs[-2], refs[-1]
    per = CORES * YS
    z = lax.axis_index("ep") // per
    copies = []
    for piece in pieces:
        for k in range(piece.shape[0] // per):
            owner = z ^ TOWER[len(copies)]
            rows = pl.ds(pl.multiple_of(owner * per, per), per)
            copies.append(pltpu.make_async_copy(piece.at[pl.ds(k * per, per), :], out.at[rows, :], sems.at[len(copies)]))
    run(copies)


def body(w_down, avg_down, router_weight, router_gain):
    _, rows, cols = w_down.shape
    groups = rows // LANES
    nc, na = 4 * LANES, LANES + HALF
    nb = nc
    at_a, at_b, at_d = nc, nc + na, nc + na + nb
    xs, eps = lax.axis_size("fsdp"), lax.axis_size("ep")
    per, part = CORES * YS, cols // LANES

    def move(v, axis, to):
        return lax.ppermute(v, axis, [(i, to(i)) for i in range(lax.axis_size(axis))])

    def shift(v, by):
        return move(v, "fsdp", lambda i: (i + by) % xs)

    def swap(v, step):
        return stacked(v, move(v, "ep", lambda e: e ^ step))

    def front(start, count, chunks, router):
        refs = [in_hbm(w_down), in_hbm(avg_down)]
        if router:
            refs += [in_hbm(router_weight.reshape(1, -1)), in_hbm(router_gain.reshape(1, -1))]
        return call(
            functools.partial(fresh_kernel, start, count, chunks, router),
            refs, [ANY] * len(refs),
            (
                pltpu.VMEM((count * LANES, cols), F32), pltpu.VMEM((count + part * router, LANES), F32),
                *(pltpu.VMEM((end - first, cols), BF16) for first, end in chunks),
            ),
            (VM,) * (2 + len(chunks)),
            [
                pltpu.VMEM((count * LANES, cols), F32), pltpu.VMEM((count * LANES, cols), F32), pltpu.VMEM((2, cols), F32),
                pltpu.SemaphoreType.DMA((2, count)), pltpu.SemaphoreType.DMA((2,)),
            ],
        )

    first = nc // LANES
    fresh_c, top_c, c = front(0, first, ((0, nc),), False)
    c_r, c_l = shift(c, 1), shift(c, -1)
    fresh_r, top_r, a, bd = front(nc, groups - first, ((0, na), (na, rows - nc)), True)
    msg = stacked(top_c, top_r)
    m2, m1, m3 = shift(msg, 2), shift(msg, 1), shift(msg, -1)
    msgs = [msg, m1, m2, m3]
    a_r, bd_l = shift(a, 1), shift(bd, -1)
    bd_r, a_l = shift(bd, 1), shift(a, -1)
    c_rr, a_rr = shift(c_r, 1), shift(a_r, 1)
    b_ll, d_ll = shift(bd_l[:nb], -1), shift(bd_l[nb:], -1)

    out, fresh_out, scale_out = call(
        functools.partial(own_kernel, groups, nc),
        [in_vmem(v) for v in (*msgs, fresh_c, fresh_r)], [VM] * 6,
        (pltpu.HBM((1, rows, cols * xs), BF16), pltpu.HBM((1, rows, cols), F32), pltpu.HBM((1, rows), F32)), (ANY,) * 3,
        [pltpu.VMEM((1, rows), F32), pltpu.VMEM((rows, cols), BF16), pltpu.SemaphoreType.DMA((4,))],
    )
    out = land(out, msgs, [c_r, c_l], [(1, 0), (3, 0)])
    out = land(out, msgs, [a_r, bd_l], [(1, at_a), (3, at_b)])
    out = land(out, msgs, [bd_r, a_l], [(1, at_b), (3, at_a)])
    out = land(out, msgs, [c_rr, b_ll], [(2, 0), (2, at_b)])
    out = land(out, msgs, [a_rr, d_ll], [(2, at_a), (2, at_d)])

    lines = stacked(stacked(msg[groups:], m1[groups:]), stacked(m2[groups:], m3[groups:]))
    lines = swap(lines, 1)
    lines = swap(lines, CORES)
    lines = swap(lines, CORES * 3)
    block = call(
        functools.partial(router_rows_kernel, part),
        [in_vmem(lines)], [VM],
        pltpu.VMEM((per, cols * xs), BF16), VM, [pltpu.VMEM((per * xs * part, LANES), F32)],
    )
    two = move(block, "ep", lambda e: e ^ per)
    both = stacked(block, two)
    four = move(both, "ep", lambda e: e ^ (per * 2))
    both = stacked(both, four)
    eight = move(both, "ep", lambda e: e ^ (per * 7))
    router = call(
        router_place_kernel,
        [in_vmem(both), in_vmem(eight)], [VM] * 2,
        pltpu.HBM((eps, cols * xs), BF16), ANY, [pltpu.SemaphoreType.DMA((ZS,))],
    )
    return out, scale_out, router.T, fresh_out


def solution(mesh):
    placed = (P("ep", None, "fsdp"), P("ep", None, "fsdp"), P("fsdp", "ep"), P("fsdp"))
    return jax.shard_map(
        body,
        mesh=mesh,
        in_specs=placed,
        out_specs=(P("ep", None, None), P("ep", None), P(), P("ep", None, "fsdp")),
        check_vma=False,
    )
```

time: 61.8 us -> 77.3 us (1.25)
  the two profiles are of different devices: /device:TPU:134 before, /device:TPU:16 now
where the time goes in v4:
time: 77.3 us; the launch traced here: 77.2 us
  waiting for transfers between devices  32.6 us (42%)
  starting transfers between devices  28.4 us (37%)
  Pallas kernels  15.1 us (20%)
  between operations  0.97 us (1%)
    ppermute x19, waiting for transfers between devices, move(): lax.ppermute(v, axis, [(i, to(i)) for i in range(lax.axis_size(axis))])  32.6 us
    ppermute x19, starting transfers between devices, move(): lax.ppermute(v, axis, [(i, to(i)) for i in range(lax.axis_size(axis))])  28.4 us
    pallas_call x10, Pallas kernels, call(): pl.pallas_call(kernel, out_shape=outs, in_specs=in_specs, out_specs=out_s...  15.1 us
  transfers between devices with their start and end apart: 19, of which 9 were waited for; matrix products, arithmetic and copies ran while one was open for 0% of the time, Pallas kernels for 11%

profile of v4, /device:TPU:16, one launch (start us, length us, event | category | flops | bytes accessed | tf_op | source)
XLA Modules:
  0.0 77.2 jit_solution(9832667725345149778)
XLA Ops:
  0.6 2.2 %shard_map.75 = (f32[512,512]{1,0:T(8,128)S(1)}, f32[4,128]{1,0:T(4,128)S(1)}, bf16[512,512]{1,0:T(8,128)(2,1)S(1)}) custom-call(f32[1,1408,512]{2,1,0:T(8,128)} %w_hbm.3, f32[1,1408,512]{2,1,0:T(8,128)} %a_hbm.3), custom_call_target="tpu_custom_call" | custom-call | tf_op jit(solution)/shard_map/pallas_call | solution.py:32
  2.8 3.1 %shard_map.76 = (f32[896,512]{1,0:T(8,128)S(1)}, f32[11,128]{1,0:T(8,128)S(1)}, bf16[192,512]{1,0:T(8,128)(2,1)S(1)}, bf16[704,512]{1,0:T(8,128)(2,1)S(1)}) custom-call(f32[1,1408,512]{2,1,0:T(8,128)} %w_hbm.3, f32[1,1408,512]{2,1,0:T(8,128)} %a_hbm.3, f32[1,512]{1,0:T(1,128)} %bitcast.4, f32[1,512]{1,0:T(1,128)} %bitcast.5), custom_call_target="tpu_custom_call" | custom-call | tf_op jit(solution)/shard_map/pallas_call | solution.py:32
  5.9 1.6 %collective-permute-start = (f32[15,128]{1,0:T(8,128)S(1)}, f32[15,128]{1,0:T(8,128)S(1)}, u32[]{:S(2)}, u32[]{:S(2)}) collective-permute-start(f32[15,128]{1,0:T(8,128)S(1)} %pad_maximum_fusion.5.m0), channel_id=1, source_target_pairs={{0,1},{1,2},{2,3},{3,0},{4,5},{5,6},{6,7},{7,4},{8,9},{9,10},{10,1... | collective-permute-start | bytes 23048 | tf_op jit(solution)/shard_map/ppermute | solution.py:228
  7.5 2.7 %collective-permute-start.1 = (f32[15,128]{1,0:T(8,128)S(1)}, f32[15,128]{1,0:T(8,128)S(1)}, u32[]{:S(2)}, u32[]{:S(2)}) collective-permute-start(f32[15,128]{1,0:T(8,128)S(1)} %pad_maximum_fusion.5.m0), channel_id=1, source_target_pairs={{0,2},{1,3},{2,0},{3,1},{4,6},{5,7},{6,4},{7,5},{8,10},{9,11},{10,... | collective-permute-start | bytes 23048 | tf_op jit(solution)/shard_map/ppermute | solution.py:228
  10.2 1.4 %collective-permute-start.2 = (f32[15,128]{1,0:T(8,128)S(1)}, f32[15,128]{1,0:T(8,128)S(1)}, u32[]{:S(2)}, u32[]{:S(2)}) collective-permute-start(f32[15,128]{1,0:T(8,128)S(1)} %pad_maximum_fusion.5.m0), channel_id=1, source_target_pairs={{0,3},{1,0},{2,1},{3,2},{4,7},{5,4},{6,5},{7,6},{8,11},{9,8},{10,9... | collective-permute-start | bytes 23048 | tf_op jit(solution)/shard_map/ppermute | solution.py:228
  11.7 0.9 %collective-permute-done.1.m2 = f32[15,128]{1,0:T(8,128)S(1)} collective-permute-done((f32[15,128]{1,0:T(8,128)S(1)}, f32[15,128]{1,0:T(8,128)S(1)}, u32[]{:S(2)}, u32[]{:S(2)}) %collective-permute-start.1) | collective-permute-done | bytes 7712 | tf_op jit(solution)/shard_map/ppermute | solution.py:228
  12.7 1.3 %collective-permute-done.2.m3 = f32[15,128]{1,0:T(8,128)S(1)} collective-permute-done((f32[15,128]{1,0:T(8,128)S(1)}, f32[15,128]{1,0:T(8,128)S(1)}, u32[]{:S(2)}, u32[]{:S(2)}) %collective-permute-start.2) | collective-permute-done | bytes 7712 | tf_op jit(solution)/shard_map/ppermute | solution.py:228
  14.1 1.2 %collective-permute-done.13 = f32[16,128]{1,0:T(8,128)S(1)} collective-permute-done((f32[16,128]{1,0:T(8,128)S(1)}, f32[16,128]{1,0:T(8,128)S(1)}, u32[]{:S(2)}, u32[]{:S(2)}) %collective-permute-start.13) | collective-permute-done | bytes 8224 | tf_op jit(solution)/shard_map/ppermute | solution.py:228
  15.3 1.3 %collective-permute-start.14 = (f32[32,128]{1,0:T(8,128)S(1)}, f32[32,128]{1,0:T(8,128)S(1)}, u32[]{:S(2)}, u32[]{:S(2)}) collective-permute-start(f32[32,128]{1,0:T(8,128)S(1)} %pad_maximum_fusion.4), channel_id=1, source_target_pairs={{0,8},{4,12},{8,0},{12,4},{16,24},{20,28},{24,16},{28,20},{32,40},... | collective-permute-start | bytes 49160 | tf_op jit(solution)/shard_map/ppermute | solution.py:228
  16.8 2.2 %collective-permute-done.14 = f32[32,128]{1,0:T(8,128)S(1)} collective-permute-done((f32[32,128]{1,0:T(8,128)S(1)}, f32[32,128]{1,0:T(8,128)S(1)}, u32[]{:S(2)}, u32[]{:S(2)}) %collective-permute-start.14) | collective-permute-done | bytes 16416 | tf_op jit(solution)/shard_map/ppermute | solution.py:228
  19.0 0.4 collective-permute-start.15
  19.5 3.5 %collective-permute-done.15 = f32[64,128]{1,0:T(8,128)S(1)} collective-permute-done((f32[64,128]{1,0:T(8,128)S(1)}, f32[64,128]{1,0:T(8,128)S(1)}, u32[]{:S(2)}, u32[]{:S(2)}) %collective-permute-start.15) | collective-permute-done | bytes 32800 | tf_op jit(solution)/shard_map/ppermute | solution.py:228
  23.0 2.0 %collective-permute-start.16 = (bf16[8,2048]{1,0:T(8,128)(2,1)S(1)}, bf16[8,2048]{1,0:T(8,128)(2,1)S(1)}, u32[]{:S(2)}, u32[]{:S(2)}) collective-permute-start(bf16[8,2048]{1,0:T(8,128)(2,1)S(1)} %shard_map.83), channel_id=1, source_target_pairs={{0,32},{4,36},{8,40},{12,44},{16,48},{20,52},{24,56},{28,60},{32,0... | collective-permute-start | bytes 98312 | tf_op jit(solution)/shard_map/ppermute | solution.py:228
  25.0 2.6 %collective-permute-start.12 = (bf16[512,512]{1,0:T(8,128)(2,1)S(1)}, bf16[512,512]{1,0:T(8,128)(2,1)S(1)}, u32[]{:S(2)}, u32[]{:S(2)}) collective-permute-start(bf16[512,512]{1,0:T(8,128)(2,1)S(1)} %get-tuple-element.18), channel_id=1, source_target_pairs={{0,3},{1,0},{2,1},{3,2},{4,7},{5,4},{6,5},{7,6},{8,11},{9,8},{10,9... | collective-permute-start | bytes 1572872 | tf_op jit(solution)/shard_map/ppermute | solution.py:228
  27.7 3.0 %collective-permute-done.5.refs_1_ = bf16[704,512]{1,0:T(8,128)(2,1)S(1)} collective-permute-done((bf16[704,512]{1,0:T(8,128)(2,1)S(1)}, bf16[704,512]{1,0:T(8,128)(2,1)S(1)}, u32[]{:S(2)}, u32[]{:S(2)}) %collective-permute-start.5) | collective-permute-done | bytes 720928 | tf_op jit(solution)/shard_map/ppermute | solution.py:228
  30.7 3.3 %collective-permute-start.17 = (bf16[16,2048]{1,0:T(8,128)(2,1)S(1)}, bf16[16,2048]{1,0:T(8,128)(2,1)S(1)}, u32[]{:S(2)}, u32[]{:S(2)}) collective-permute-start(bf16[16,2048]{1,0:T(8,128)(2,1)S(1)} %pad_maximum_fusion.1), channel_id=1, source_target_pairs={{0,64},{4,68},{8,72},{12,76},{16,80},{20,84},{24,88},{28,92},{32,9... | collective-permute-start | bytes 196616 | tf_op jit(solution)/shard_map/ppermute | solution.py:228
  34.0 2.2 %collective-permute-done.17 = bf16[16,2048]{1,0:T(8,128)(2,1)S(1)} collective-permute-done((bf16[16,2048]{1,0:T(8,128)(2,1)S(1)}, bf16[16,2048]{1,0:T(8,128)(2,1)S(1)}, u32[]{:S(2)}, u32[]{:S(2)}) %collective-permute-start.17) | collective-permute-done | bytes 65568 | tf_op jit(solution)/shard_map/ppermute | solution.py:228
  36.2 0.4 collective-permute-start.11
  36.6 1.6 %collective-permute-start.8 = (bf16[512,512]{1,0:T(8,128)(2,1)S(1)}, bf16[512,512]{1,0:T(8,128)(2,1)S(1)}, u32[]{:S(2)}, u32[]{:S(2)}) collective-permute-start(bf16[512,512]{1,0:T(8,128)(2,1)S(1)} %collective-permute-done.7.refs_0_), channel_id=1, source_target_pairs={{0,1},{1,2},{2,3},{3,0},{4,5},{5,6},{6,7},{7,4},{8,9},{9,10},{10,1... | collective-permute-start | bytes 1572872 | tf_op jit(solution)/shard_map/ppermute | solution.py:228
  38.2 14.0 %collective-permute-done.3.refs_0_ = bf16[192,512]{1,0:T(8,128)(2,1)S(1)} collective-permute-done((bf16[192,512]{1,0:T(8,128)(2,1)S(1)}, bf16[192,512]{1,0:T(8,128)(2,1)S(1)}, u32[]{:S(2)}, u32[]{:S(2)}) %collective-permute-start.3) | collective-permute-done | bytes 196640 | tf_op jit(solution)/shard_map/ppermute | solution.py:228
  52.2 1.4 %collective-permute-start.9 = (bf16[512,512]{1,0:T(8,128)(2,1)S(1)}, bf16[512,512]{1,0:T(8,128)(2,1)S(1)}, u32[]{:S(2)}, u32[]{:S(2)}) collective-permute-start(bf16[512,512]{1,0:T(8,128)(2,1)S(1)} %slice.25), channel_id=1, source_target_pairs={{0,3},{1,0},{2,1},{3,2},{4,7},{5,4},{6,5},{7,6},{8,11},{9,8},{10,9... | collective-permute-start | bytes 1572872 | tf_op jit(solution)/shard_map/ppermute | solution.py:228
  53.7 5.9 %collective-permute-start.18 = (bf16[32,2048]{1,0:T(8,128)(2,1)S(1)}, bf16[32,2048]{1,0:T(8,128)(2,1)S(1)}, u32[]{:S(2)}, u32[]{:S(2)}) collective-permute-start(bf16[32,2048]{1,0:T(8,128)(2,1)S(1)} %pad_maximum_fusion.refs_0_), channel_id=1, source_target_pairs={{0,224},{4,228},{8,232},{12,236},{16,240},{20,244},{24,248},{28,25... | collective-permute-start | bytes 393224 | tf_op jit(solution)/shard_map/ppermute | solution.py:228
  59.6 4.3 %collective-permute-done.18.refs_1_ = bf16[32,2048]{1,0:T(8,128)(2,1)S(1)} collective-permute-done((bf16[32,2048]{1,0:T(8,128)(2,1)S(1)}, bf16[32,2048]{1,0:T(8,128)(2,1)S(1)}, u32[]{:S(2)}, u32[]{:S(2)}) %collective-permute-start.18) | collective-permute-done | bytes 131104 | tf_op jit(solution)/shard_map/ppermute | solution.py:228
  64.0 0.6 collective-permute-start.4
  64.6 2.6 %collective-permute-start.6 = (bf16[192,512]{1,0:T(8,128)(2,1)S(1)}, bf16[192,512]{1,0:T(8,128)(2,1)S(1)}, u32[]{:S(2)}, u32[]{:S(2)}) collective-permute-start(bf16[192,512]{1,0:T(8,128)(2,1)S(1)} %slice.24), channel_id=1, source_target_pairs={{0,3},{1,0},{2,1},{3,2},{4,7},{5,4},{6,5},{7,6},{8,11},{9,8},{10,9... | collective-permute-start | bytes 589832 | tf_op jit(solution)/shard_map/ppermute | solution.py:228
  67.2 2.1 %shard_map.77 = (bf16[1,1408,2048]{2,1,0:T(8,128)(2,1)}, f32[1,1408,512]{2,1,0:T(8,128)}, f32[1,1408]{1,0:T(1,128)}) custom-call(f32[15,128]{1,0:T(8,128)S(1)} %pad_maximum_fusion.5.m0, f32[15,128]{1,0:T(8,128)S(1)} %collective-permute-done.m1, f32[15,128]{1,0:T(8,128)S(1)} %collective-permute-done.1.m2, f32[15,128]{1,0:T(8,128)S(1)} %collective-permute-done.2.m3, ...), custom_call_target="tpu_custom_call" | custom-call | tf_op jit(solution)/shard_map/pallas_call | solution.py:32
  69.3 0.8 %shard_map.84 = bf16[64,2048]{1,0:T(8,128)(2,1)} custom-call(bf16[32,2048]{1,0:T(8,128)(2,1)S(1)} %pad_maximum_fusion.refs_0_, bf16[32,2048]{1,0:T(8,128)(2,1)S(1)} %collective-permute-done.18.refs_1_), custom_call_target="tpu_custom_call" | custom-call | tf_op jit(solution)/shard_map/pallas_call | solution.py:32
  70.1 1.5 %shard_map.78.refs_2_ = bf16[1,1408,2048]{2,1,0:T(8,128)(2,1)} custom-call(f32[15,128]{1,0:T(8,128)S(1)} %pad_maximum_fusion.5.m0, f32[15,128]{1,0:T(8,128)S(1)} %collective-permute-done.m1, f32[15,128]{1,0:T(8,128)S(1)} %collective-permute-done.1.m2, f32[15,128]{1,0:T(8,128)S(1)} %collective-permute-done.2.m3, ...), custom_call_target="tpu_custom_call", output_to_operand_aliasing={{}: (6, {})} | custom-call | tf_op jit(solution)/shard_map/pallas_call | solution.py:32
  71.6 1.5 %shard_map.79.refs_2_ = bf16[1,1408,2048]{2,1,0:T(8,128)(2,1)} custom-call(f32[15,128]{1,0:T(8,128)S(1)} %pad_maximum_fusion.5.m0, f32[15,128]{1,0:T(8,128)S(1)} %collective-permute-done.m1, f32[15,128]{1,0:T(8,128)S(1)} %collective-permute-done.1.m2, f32[15,128]{1,0:T(8,128)S(1)} %collective-permute-done.2.m3, ...), custom_call_target="tpu_custom_call", output_to_operand_aliasing={{}: (6, {})} | custom-call | tf_op jit(solution)/shard_map/pallas_call | solution.py:32
  73.1 1.5 %shard_map.80.refs_2_ = bf16[1,1408,2048]{2,1,0:T(8,128)(2,1)} custom-call(f32[15,128]{1,0:T(8,128)S(1)} %pad_maximum_fusion.5.m0, f32[15,128]{1,0:T(8,128)S(1)} %collective-permute-done.m1, f32[15,128]{1,0:T(8,128)S(1)} %collective-permute-done.1.m2, f32[15,128]{1,0:T(8,128)S(1)} %collective-permute-done.2.m3, ...), custom_call_target="tpu_custom_call", output_to_operand_aliasing={{}: (6, {})} | custom-call | tf_op jit(solution)/shard_map/pallas_call | solution.py:32
  74.5 1.5 %shard_map.81.refs_2_ = bf16[1,1408,2048]{2,1,0:T(8,128)(2,1)} custom-call(f32[15,128]{1,0:T(8,128)S(1)} %pad_maximum_fusion.5.m0, f32[15,128]{1,0:T(8,128)S(1)} %collective-permute-done.m1, f32[15,128]{1,0:T(8,128)S(1)} %collective-permute-done.1.m2, f32[15,128]{1,0:T(8,128)S(1)} %collective-permute-done.2.m3, ...), custom_call_target="tpu_custom_call", output_to_operand_aliasing={{}: (6, {})} | custom-call | tf_op jit(solution)/shard_map/pallas_call | solution.py:32
  76.1 1.0 %shard_map.82 = bf16[1,1408,2048]{2,1,0:T(8,128)(2,1)} custom-call(f32[15,128]{1,0:T(8,128)S(1)} %pad_maximum_fusion.5.m0, f32[15,128]{1,0:T(8,128)S(1)} %collective-permute-done.m1, f32[15,128]{1,0:T(8,128)S(1)} %collective-permute-done.1.m2, f32[15,128]{1,0:T(8,128)S(1)} %collective-permute-done.2.m3, ...), custom_call_target="tpu_custom_call", output_to_operand_aliasing={{}: (6, {})} | custom-call | tf_op jit(solution)/shard_map/pallas_call | solution.py:32
  (29 shorter events, 0.6 us)
Async XLA Ops:
  5.9 5.8 %collective-permute-start = (f32[15,128]{1,0:T(8,128)S(1)}, f32[15,128]{1,0:T(8,128)S(1)}, u32[]{:S(2)}, u32[]{:S(2)}) collective-permute-start(f32[15,128]{1,0:T(8,128)S(1)} %pad_maximum_fusion.5.m0), channel_id=1, source_target_pairs={{0,1},{1,2},{2,3},{3,0},{4,5},{5,6},{6,7},{7,4},{8,9},{9,10},{10,1... | collective-permute-start | bytes 23048 | tf_op jit(solution)/shard_map/ppermute | solution.py:228
  7.5 5.2 %collective-permute-start.1 = (f32[15,128]{1,0:T(8,128)S(1)}, f32[15,128]{1,0:T(8,128)S(1)}, u32[]{:S(2)}, u32[]{:S(2)}) collective-permute-start(f32[15,128]{1,0:T(8,128)S(1)} %pad_maximum_fusion.5.m0), channel_id=1, source_target_pairs={{0,2},{1,3},{2,0},{3,1},{4,6},{5,7},{6,4},{7,5},{8,10},{9,11},{10,... | collective-permute-start | bytes 23048 | tf_op jit(solution)/shard_map/ppermute | solution.py:228
  10.2 3.7 %collective-permute-start.2 = (f32[15,128]{1,0:T(8,128)S(1)}, f32[15,128]{1,0:T(8,128)S(1)}, u32[]{:S(2)}, u32[]{:S(2)}) collective-permute-start(f32[15,128]{1,0:T(8,128)S(1)} %pad_maximum_fusion.5.m0), channel_id=1, source_target_pairs={{0,3},{1,0},{2,1},{3,2},{4,7},{5,4},{6,5},{7,6},{8,11},{9,8},{10,9... | collective-permute-start | bytes 23048 | tf_op jit(solution)/shard_map/ppermute | solution.py:228
  11.7 19.0 %collective-permute-start.5 = (bf16[704,512]{1,0:T(8,128)(2,1)S(1)}, bf16[704,512]{1,0:T(8,128)(2,1)S(1)}, u32[]{:S(2)}, u32[]{:S(2)}) collective-permute-start(bf16[704,512]{1,0:T(8,128)(2,1)S(1)} %get-tuple-element.17), channel_id=1, source_target_pairs={{0,3},{1,0},{2,1},{3,2},{4,7},{5,4},{6,5},{7,6},{8,11},{9,8},{10,9... | collective-permute-start | bytes 2162696 | tf_op jit(solution)/shard_map/ppermute | solution.py:228
  14.0 1.3 %collective-permute-start.13 = (f32[16,128]{1,0:T(8,128)S(1)}, f32[16,128]{1,0:T(8,128)S(1)}, u32[]{:S(2)}, u32[]{:S(2)}) collective-permute-start(f32[16,128]{1,0:T(8,128)S(1)} %fusion), channel_id=1, source_target_pairs={{0,4},{4,0},{8,12},{12,8},{16,20},{20,16},{24,28},{28,24},{32,36},... | collective-permute-start | bytes 24584 | tf_op jit(solution)/shard_map/ppermute | solution.py:228
  15.3 3.7 %collective-permute-start.14 = (f32[32,128]{1,0:T(8,128)S(1)}, f32[32,128]{1,0:T(8,128)S(1)}, u32[]{:S(2)}, u32[]{:S(2)}) collective-permute-start(f32[32,128]{1,0:T(8,128)S(1)} %pad_maximum_fusion.4), channel_id=1, source_target_pairs={{0,8},{4,12},{8,0},{12,4},{16,24},{20,28},{24,16},{28,20},{32,40},... | collective-permute-start | bytes 49160 | tf_op jit(solution)/shard_map/ppermute | solution.py:228
  16.5 20.1 %collective-permute-start.7 = (bf16[512,512]{1,0:T(8,128)(2,1)S(1)}, bf16[512,512]{1,0:T(8,128)(2,1)S(1)}, u32[]{:S(2)}, u32[]{:S(2)}) collective-permute-start(bf16[512,512]{1,0:T(8,128)(2,1)S(1)} %get-tuple-element.18), channel_id=1, source_target_pairs={{0,1},{1,2},{2,3},{3,0},{4,5},{5,6},{6,7},{7,4},{8,9},{9,10},{10,1... | collective-permute-start | bytes 1572872 | tf_op jit(solution)/shard_map/ppermute | solution.py:228
  19.0 3.9 %collective-permute-start.15 = (f32[64,128]{1,0:T(8,128)S(1)}, f32[64,128]{1,0:T(8,128)S(1)}, u32[]{:S(2)}, u32[]{:S(2)}) collective-permute-start(f32[64,128]{1,0:T(8,128)S(1)} %pad_maximum_fusion.3), channel_id=1, source_target_pairs={{0,24},{4,28},{8,16},{12,20},{16,8},{20,12},{24,0},{28,4},{32,56},... | collective-permute-start | bytes 98312 | tf_op jit(solution)/shard_map/ppermute | solution.py:228
  23.0 4.7 %collective-permute-start.16 = (bf16[8,2048]{1,0:T(8,128)(2,1)S(1)}, bf16[8,2048]{1,0:T(8,128)(2,1)S(1)}, u32[]{:S(2)}, u32[]{:S(2)}) collective-permute-start(bf16[8,2048]{1,0:T(8,128)(2,1)S(1)} %shard_map.83), channel_id=1, source_target_pairs={{0,32},{4,36},{8,40},{12,44},{16,48},{20,52},{24,56},{28,60},{32,0... | collective-permute-start | bytes 98312 | tf_op jit(solution)/shard_map/ppermute | solution.py:228
  25.0 39.6 %collective-permute-start.12 = (bf16[512,512]{1,0:T(8,128)(2,1)S(1)}, bf16[512,512]{1,0:T(8,128)(2,1)S(1)}, u32[]{:S(2)}, u32[]{:S(2)}) collective-permute-start(bf16[512,512]{1,0:T(8,128)(2,1)S(1)} %get-tuple-element.18), channel_id=1, source_target_pairs={{0,3},{1,0},{2,1},{3,2},{4,7},{5,4},{6,5},{7,6},{8,11},{9,8},{10,9... | collective-permute-start | bytes 1572872 | tf_op jit(solution)/shard_map/ppermute | solution.py:228
  27.7 45.4 %collective-permute-start.10 = (bf16[704,512]{1,0:T(8,128)(2,1)S(1)}, bf16[704,512]{1,0:T(8,128)(2,1)S(1)}, u32[]{:S(2)}, u32[]{:S(2)}) collective-permute-start(bf16[704,512]{1,0:T(8,128)(2,1)S(1)} %get-tuple-element.17), channel_id=1, source_target_pairs={{0,1},{1,2},{2,3},{3,0},{4,5},{5,6},{6,7},{7,4},{8,9},{9,10},{10,1... | collective-permute-start | bytes 2162696 | tf_op jit(solution)/shard_map/ppermute | solution.py:228
  27.7 24.5 %collective-permute-start.3 = (bf16[192,512]{1,0:T(8,128)(2,1)S(1)}, bf16[192,512]{1,0:T(8,128)(2,1)S(1)}, u32[]{:S(2)}, u32[]{:S(2)}) collective-permute-start(bf16[192,512]{1,0:T(8,128)(2,1)S(1)} %get-tuple-element.16), channel_id=1, source_target_pairs={{0,1},{1,2},{2,3},{3,0},{4,5},{5,6},{6,7},{7,4},{8,9},{9,10},{10,1... | collective-permute-start | bytes 589832 | tf_op jit(solution)/shard_map/ppermute | solution.py:228
  30.7 5.5 %collective-permute-start.17 = (bf16[16,2048]{1,0:T(8,128)(2,1)S(1)}, bf16[16,2048]{1,0:T(8,128)(2,1)S(1)}, u32[]{:S(2)}, u32[]{:S(2)}) collective-permute-start(bf16[16,2048]{1,0:T(8,128)(2,1)S(1)} %pad_maximum_fusion.1), channel_id=1, source_target_pairs={{0,64},{4,68},{8,72},{12,76},{16,80},{20,84},{24,88},{28,92},{32,9... | collective-permute-start | bytes 196616 | tf_op jit(solution)/shard_map/ppermute | solution.py:228
  36.2 17.5 %collective-permute-start.11 = (bf16[192,512]{1,0:T(8,128)(2,1)S(1)}, bf16[192,512]{1,0:T(8,128)(2,1)S(1)}, u32[]{:S(2)}, u32[]{:S(2)}) collective-permute-start(bf16[192,512]{1,0:T(8,128)(2,1)S(1)} %get-tuple-element.16), channel_id=1, source_target_pairs={{0,3},{1,0},{2,1},{3,2},{4,7},{5,4},{6,5},{7,6},{8,11},{9,8},{10,9... | collective-permute-start | bytes 589832 | tf_op jit(solution)/shard_map/ppermute | solution.py:228
  36.6 37.9 %collective-permute-start.8 = (bf16[512,512]{1,0:T(8,128)(2,1)S(1)}, bf16[512,512]{1,0:T(8,128)(2,1)S(1)}, u32[]{:S(2)}, u32[]{:S(2)}) collective-permute-start(bf16[512,512]{1,0:T(8,128)(2,1)S(1)} %collective-permute-done.7.refs_0_), channel_id=1, source_target_pairs={{0,1},{1,2},{2,3},{3,0},{4,5},{5,6},{6,7},{7,4},{8,9},{9,10},{10,1... | collective-permute-start | bytes 1572872 | tf_op jit(solution)/shard_map/ppermute | solution.py:228
  52.2 22.3 %collective-permute-start.9 = (bf16[512,512]{1,0:T(8,128)(2,1)S(1)}, bf16[512,512]{1,0:T(8,128)(2,1)S(1)}, u32[]{:S(2)}, u32[]{:S(2)}) collective-permute-start(bf16[512,512]{1,0:T(8,128)(2,1)S(1)} %slice.25), channel_id=1, source_target_pairs={{0,3},{1,0},{2,1},{3,2},{4,7},{5,4},{6,5},{7,6},{8,11},{9,8},{10,9... | collective-permute-start | bytes 1572872 | tf_op jit(solution)/shard_map/ppermute | solution.py:228
  53.7 10.3 %collective-permute-start.18 = (bf16[32,2048]{1,0:T(8,128)(2,1)S(1)}, bf16[32,2048]{1,0:T(8,128)(2,1)S(1)}, u32[]{:S(2)}, u32[]{:S(2)}) collective-permute-start(bf16[32,2048]{1,0:T(8,128)(2,1)S(1)} %pad_maximum_fusion.refs_0_), channel_id=1, source_target_pairs={{0,224},{4,228},{8,232},{12,236},{16,240},{20,244},{24,248},{28,25... | collective-permute-start | bytes 393224 | tf_op jit(solution)/shard_map/ppermute | solution.py:228
  64.0 12.1 %collective-permute-start.4 = (bf16[192,512]{1,0:T(8,128)(2,1)S(1)}, bf16[192,512]{1,0:T(8,128)(2,1)S(1)}, u32[]{:S(2)}, u32[]{:S(2)}) collective-permute-start(bf16[192,512]{1,0:T(8,128)(2,1)S(1)} %collective-permute-done.3.refs_0_), channel_id=1, source_target_pairs={{0,1},{1,2},{2,3},{3,0},{4,5},{5,6},{6,7},{7,4},{8,9},{9,10},{10,1... | collective-permute-start | bytes 589832 | tf_op jit(solution)/shard_map/ppermute | solution.py:228
  64.6 11.5 %collective-permute-start.6 = (bf16[192,512]{1,0:T(8,128)(2,1)S(1)}, bf16[192,512]{1,0:T(8,128)(2,1)S(1)}, u32[]{:S(2)}, u32[]{:S(2)}) collective-permute-start(bf16[192,512]{1,0:T(8,128)(2,1)S(1)} %slice.24), channel_id=1, source_target_pairs={{0,3},{1,0},{2,1},{3,2},{4,7},{5,4},{6,5},{7,6},{8,11},{9,8},{10,9... | collective-permute-start | bytes 589832 | tf_op jit(solution)/shard_map/ppermute | solution.py:228
